TPU v7x, 32 devices: a whole 2x2x4 slice. The times are simulated.
32 devices in a mesh: win: 2 (over y), dx: 4 (over z), dy: 2 (over x), dz: 2 (over core).
Axes of the slice: x: 2, y: 2, z: 4, core: 2. Of those that a mesh axis runs over, the one named last changes fastest.
Arguments:
- fraction: float32 [3, 8, 2, 2, 768], P(None, ('win', 'dx'), 'dy', 'dz'), parts along dimension 1, may hold values from 0 to 1
- atom_type: int32 [8, 2, 2, 768], P(('win', 'dx'), 'dy', 'dz'), parts along dimension 0, may hold values from 0 to 31
- perturbed: int32 [8, 2, 2, 768], P(('win', 'dx'), 'dy', 'dz'), parts along dimension 0, may hold values from 0 to 1
- leaving: int32 [8, 2, 2, 2, 16], P(('win', 'dx'), 'dy', 'dz'), parts along dimension 0, may hold values from 0 to 767, as said below
- neighbours: int32 [8, 2, 2, 6, 16], P(('win', 'dx'), 'dy', 'dz'), parts along dimension 0, may hold values from 0 to 161, as said below
- counts: int32 [8, 2, 2, 6], P(('win', 'dx'), 'dy', 'dz'), parts along dimension 0, may hold values from 1 to 16, as said below
- sigma_table: float32 [32], replicated, may hold values from 0.8 to 1.2
- depth_table: float32 [32], replicated, may hold values from 0.002 to 0.03
- charge_table: float32 [32], replicated, may hold values from -1 to 1
- domain_edge: float32 [3], replicated, may hold values from 1 to 1.12
- coupling: float32 [2], P('win'), parts along dimension 0, may hold values from 0.1 to 0.9
Outputs:
- forces: float32 [3, 8, 2, 2, 768], P(None, ('win', 'dx'), 'dy', 'dz'), parts along dimension 1
- energy: float32 [2], P('win'), parts along dimension 0
- dhdl: float32 [2], P('win'), parts along dimension 0
There are 2 independent parts, one for each index of `win`. A program takes and returns all parts, laid end to end along the dimension named above; an argument that names none is the same for every part. Nothing has to cross between parts.
Inputs may be any that keep to these rules, and one draw needn't show every extreme that they name: `leaving`: each domain lists 2 * 16 distinct slots: the first 16 leave toward the next domain, the last 16 toward the previous one. `neighbours`: each list holds 16 distinct ghost block numbers; entries at or past the block's count are valid numbers and are not used. `counts`: some block lists exactly 16 blocks in every draw.
All inputs are finite; a program needn't handle non-finite values.
Results may differ from a plain program's by a relative error of at most 0.0003.
Values sent between devices are 32-bit elements; how exact they have to be, the bound alone decides.
A program may use at most 64 MiB of HBM per device.

v0:
```python
import jax
import jax.numpy as jnp
from jax import lax
from jax.experimental import pallas as pl
from jax.experimental.pallas import tpu as pltpu
from jax.sharding import PartitionSpec as P

soft_base = 0.3
soft_alpha = 0.5
charge_base = 0.3
charge_alpha = 0.5
coulomb = 0.1
LANES = 128
MESH = pl.DeviceIdType.MESH
HIGHEST = lax.Precision.HIGHEST


def steps_of(count):
    return {1: (0,), 2: (0, 1)}.get(count, (-1, 0, 1))


def slot_step(step, count):
    if count == 1:
        return step * 0
    if count == 2:
        return step * step
    return step + 1


def thirds(value):
    high = value.astype(jnp.bfloat16).astype(jnp.float32)
    rest = value - high
    middle = rest.astype(jnp.bfloat16).astype(jnp.float32)
    return jnp.concatenate([high, middle, rest - middle], axis=0)


def joined(value):
    return value[0:8] + value[8:16] + value[16:24]


def step_kernel(
    sizes,
    edge_ref,
    coupling_ref,
    sigma_ref,
    depth_ref,
    charge_ref,
    listed_ref,
    count_ref,
    fraction_ref,
    type_ref,
    flag_ref,
    leaving_ref,
    force_ref,
    energy_ref,
    dhdl_ref,
    ghost_ref,
    outgoing,
    incoming,
    own_cols,
    force_acc,
    params,
    sums_ref,
    tile,
    gathered,
    mig_send,
    mig_recv,
    send_sem,
    recv_sem,
    sum_send,
    sum_recv,
):
    nx, ny, nz = sizes
    atoms = fraction_ref.shape[-1]
    spacing = float(atoms) ** (1.0 / 3.0)
    me = (lax.axis_index("dx"), lax.axis_index("dy"), lax.axis_index("dz"))

    def device(step):
        return {
            name: lax.rem(place + by + count, count)
            for name, place, by, count in zip(("dx", "dy", "dz"), me, step, sizes)
        }

    offsets = [(a, b, c) for a in steps_of(nx) for b in steps_of(ny) for c in steps_of(nz)]
    others = [o for o in offsets if any(o)]

    def slot(o):
        return (
            slot_step(o[0], nx) * len(steps_of(ny)) + slot_step(o[1], ny)
        ) * len(steps_of(nz)) + slot_step(o[2], nz)

    barrier = pltpu.get_barrier_semaphore()
    total = nx * ny * nz
    my_id = (me[0] * ny + me[1]) * nz + me[2]

    def window_device(k):
        return {
            "dx": lax.div(k, ny * nz),
            "dy": lax.rem(lax.div(k, nz), ny),
            "dz": lax.rem(k, nz),
        }

    @pl.loop(1, total)
    def _(by):
        pl.semaphore_signal(
            barrier,
            inc=1,
            device_id=window_device(lax.rem(my_id + by, total)),
            device_id_type=MESH,
        )

    own = ghost_ref.at[slot((0, 0, 0))]
    edge = [edge_ref[k] * spacing for k in range(3)]
    rows = [fraction_ref[k, 0, 0] * edge[k] for k in range(3)]
    rows += [type_ref[0, 0].astype(jnp.float32), flag_ref[0, 0].astype(jnp.float32)]
    payload = jnp.concatenate(rows + [jnp.zeros((3, atoms), jnp.float32)], axis=0)
    leave = leaving_ref[0, 0, 0]
    mig = leave.shape[1]
    slots_in = jnp.concatenate([leave[0:1], leave[1:2]], axis=1)
    slots_out = jnp.concatenate([leave[1:2], leave[0:1]], axis=1)
    place = lax.broadcasted_iota(jnp.int32, (atoms, 2 * mig), 0)
    hot_in = (place == slots_in).astype(jnp.float32).astype(jnp.bfloat16)
    hot_out = (place == slots_out).astype(jnp.float32).astype(jnp.bfloat16)
    lane = lax.broadcasted_iota(jnp.int32, (8, 2 * mig), 1)
    first = lax.broadcasted_iota(jnp.int32, (8, 2 * mig), 0) == 0
    shift = jnp.where(first, jnp.where(lane < mig, edge[0], -edge[0]), 0.0)
    leavers = joined(
        jnp.dot(thirds(payload).astype(jnp.bfloat16), hot_out, preferred_element_type=jnp.float32)
    )
    outgoing[...] = leavers + shift

    def spread(value):
        return lax.dot_general(
            value.astype(jnp.bfloat16),
            hot_in,
            (((1,), (1,)), ((), ())),
            preferred_element_type=jnp.float32,
        )

    gone = spread(jnp.ones((8, 2 * mig), jnp.float32))

    pl.semaphore_wait(barrier, total - 1)
    moves = []
    for side, by in ((0, 1), (1, -1)):
        move = pltpu.make_async_remote_copy(
            src_ref=outgoing,
            dst_ref=incoming.at[side],
            send_sem=mig_send.at[side],
            recv_sem=mig_recv.at[side],
            device_id=device((by, 0, 0)),
            device_id_type=MESH,
        )
        move.start()
        moves.append(move)
    for move in moves:
        move.wait()
    merged = jnp.where(lane < mig, incoming[1], incoming[0])
    moved = jnp.where(gone > 0.5, joined(spread(thirds(merged))), payload)
    for r in range(5):
        own[r] = moved[r : r + 1]
    copies = []
    for k, o in enumerate(sorted(others, key=lambda o: -sum(map(abs, o)))):
        copy = pltpu.make_async_remote_copy(
            src_ref=own,
            dst_ref=ghost_ref.at[slot(o)],
            send_sem=send_sem.at[k],
            recv_sem=recv_sem.at[k],
            device_id=device(tuple(-x for x in o)),
            device_id_type=MESH,
        )
        copy.start()
        copies.append((copy, slot(o)))

    blocks = atoms // LANES
    lam = coupling_ref[0]
    own_slot = slot((0, 0, 0))
    ones = jnp.ones((8, LANES), jnp.bfloat16)
    for k in range(3):
        sums_ref[k] = jnp.zeros((8, LANES), jnp.float32)

    ahead = lax.broadcasted_iota(jnp.int32, (8, LANES), 1) - lax.broadcasted_iota(
        jnp.int32, (8, LANES), 0
    )
    lane = lax.broadcasted_iota(jnp.int32, (1, LANES), 1)
    tables = [jnp.zeros((1, LANES), jnp.float32)] * 3
    for k in range(sigma_ref.shape[0]):
        hit = lane == k
        tables = [
            jnp.where(hit, ref[k], table)
            for ref, table in zip((sigma_ref, depth_ref, charge_ref), tables)
        ]
    table = jnp.concatenate(
        [tables[0] * 0.5, jnp.sqrt(tables[1]) * 2.0, tables[2]] + [tables[2] * 0.0] * 5, axis=0
    )
    kinds = sigma_ref.shape[0]
    table_parts = thirds(table[:, :kinds]).astype(jnp.bfloat16)
    kind_row = lax.broadcasted_iota(jnp.int32, (kinds, atoms), 0).astype(jnp.float32)

    def look_up(place):
        onehot = (kind_row == ghost_ref[place, 3]).astype(jnp.float32).astype(jnp.bfloat16)
        found = joined(jnp.dot(table_parts, onehot, preferred_element_type=jnp.float32))
        rows = [ghost_ref[place, r] for r in range(3)]
        rows += [found[0:3], ghost_ref[place, 4], found[3:4]]
        whole = jnp.concatenate(rows, axis=0)
        for q in range(blocks):
            params[place * blocks + q] = whole[:, q * LANES : (q + 1) * LANES]

    look_up(own_slot)
    picks = (
        lax.broadcasted_iota(jnp.int32, (24, 7 * LANES), 0) % 8
        == lax.broadcasted_iota(jnp.int32, (24, 7 * LANES), 1) // LANES
    ).astype(jnp.float32).astype(jnp.bfloat16)
    for q in range(blocks):
        cols = thirds(params[own_slot * blocks + q]).T.astype(jnp.bfloat16)
        wide = jnp.dot(cols, picks, preferred_element_type=jnp.float32)
        for r in range(7):
            col = wide[:, r * LANES : (r + 1) * LANES]
            own_cols[q, r] = col * coulomb if r == 5 else col
    for q in range(blocks):
        for k in range(3):
            force_acc[q, k] = jnp.zeros((LANES, LANES), jnp.float32)

    for copy, place in copies:
        copy.wait()
        look_up(place)

    @pl.loop(0, blocks)
    def _(q):
        def entry(e):
            listed = listed_ref[q, 0, e]
            left = jnp.minimum(jnp.maximum(count_ref[0, 0, 0, q] - e, 0), 1)
            used = left.astype(jnp.float32)
            apart = jnp.abs(listed - (13 * blocks + q))
            self_lane = jnp.minimum(apart, 1) * (2 * LANES)
            image = lax.div(listed, blocks)
            a = lax.div(image, 9) - 1
            b = lax.rem(lax.div(image, 3), 3) - 1
            c = lax.rem(image, 3) - 1
            where_from = (
                slot_step(a, nx) * len(steps_of(ny)) + slot_step(b, ny)
            ) * len(steps_of(nz)) + slot_step(c, nz)
            other = params[where_from * blocks + lax.rem(listed, blocks)]
            rows = []
            for r in range(7):
                row = other[r : r + 1]
                if r < 3:
                    row = row + (a, b, c)[r].astype(jnp.float32) * edge[r]
                if 4 <= r < 6:
                    row = row * used
                rows.append(jnp.broadcast_to(row, (8, LANES)))
            xj, yj, zj, hj, ej, qj, pj = rows

            tot = jnp.zeros((8, LANES), jnp.float32)
            tot_p = jnp.zeros((8, LANES), jnp.float32)
            tot_k = jnp.zeros((8, LANES), jnp.float32)
            for g in range(LANES // 8):
                at = pl.ds(g * 8, 8)
                dx = own_cols[q, 0, at] - xj
                dy = own_cols[q, 1, at] - yj
                dz = own_cols[q, 2, at] - zj
                r2 = dx * dx + dy * dy + dz * dz
                sig = own_cols[q, 3, at] + hj
                s2 = sig * sig
                s6 = s2 * s2 * s2
                eps4 = own_cols[q, 4, at] * ej
                qq = own_cols[q, 5, at] * qj
                diag = ahead == self_lane + g * 8
                eps4 = jnp.where(diag, 0.0, eps4)
                qq = jnp.where(diag, 0.0, qq)
                p = jnp.maximum(own_cols[q, 6, at], pj)
                soft = soft_base + (soft_alpha * lam) * p
                weight = 1.0 - lam * p
                r4 = r2 * r2
                soft6 = s6 * soft + r4 * r2
                inv = 1.0 / soft6
                u = lax.rsqrt(soft + r2)
                ec = qq * u
                half = (0.5 * ec) * (u * u)
                t = s6 * inv
                et = eps4 * t
                tm = t - 1.0
                v = et * tm + ec
                m = et * (t + tm)
                kk = m * t + half
                fs = weight * (3.0 * (m * (r4 * inv)) + half)
                tot = tot + v
                tot_p = tot_p + p * v
                tot_k = tot_k + p * kk
                force_acc[q, 0, at] += fs * dx
                force_acc[q, 1, at] += fs * dy
                force_acc[q, 2, at] += fs * dz
            sums_ref[0] += tot
            sums_ref[1] += tot_p
            sums_ref[2] += tot_k

        width = listed_ref.shape[-1]
        unroll = 4 if width % 4 == 0 else 1

        @pl.loop(0, width // unroll)
        def _(step):
            for k in range(unroll):
                entry(step * unroll + k)

    folded = [jnp.sum(sums_ref[k], axis=0, keepdims=True) for k in range(3)]
    folded.append(jnp.zeros((5, LANES), jnp.float32))
    mine = jnp.concatenate(folded, axis=0)
    tile[...] = mine
    gathered[my_id] = mine

    def share(by):
        return pltpu.make_async_remote_copy(
            src_ref=tile,
            dst_ref=gathered.at[my_id],
            send_sem=sum_send.at[by],
            recv_sem=sum_recv.at[by],
            device_id=window_device(lax.rem(my_id + by, total)),
            device_id_type=MESH,
        )

    @pl.loop(1, total)
    def _(by):
        share(by).start()

    for q in range(blocks):
        for k in range(3):
            whole = force_acc[q, k]
            high = whole.astype(jnp.bfloat16)
            low = (whole - high.astype(jnp.float32)).astype(jnp.bfloat16)
            reduced = sum(
                lax.dot_general(
                    ones, part, (((1,), (1,)), ((), ())), preferred_element_type=jnp.float32
                )
                for part in (high, low)
            )
            force_ref[k, 0, 0, :, q * LANES : (q + 1) * LANES] = 2.0 * reduced[0:1]

    @pl.loop(1, total)
    def _(by):
        share(by).wait()

    summed = jnp.sum(gathered[...], axis=0)
    parts = [jnp.sum(summed[k : k + 1]) for k in range(3)]
    scale = 0.5 / float(atoms * total)
    energy_ref[0] = scale * (parts[0] - lam * parts[1])
    dhdl_ref[0] = -scale * (parts[1] + (0.5 * (1.0 - lam)) * parts[2])


def on_device(sizes, fraction, atom_type, perturbed, leaving, neighbours, counts,
              sigma_table, depth_table, charge_table, domain_edge, coupling):
    nx, ny, nz = sizes
    atoms = fraction.shape[-1]
    mig = leaving.shape[-1]
    slots = len(steps_of(nx)) * len(steps_of(ny)) * len(steps_of(nz))
    smem = pl.BlockSpec(memory_space=pltpu.SMEM)
    vmem = pl.BlockSpec(memory_space=pltpu.VMEM)
    f32 = jnp.float32

    def bound(kernel, *values):
        return lambda *refs: kernel(*values, *refs)

    blocks = atoms // LANES
    total = nx * ny * nz
    dma = pltpu.SemaphoreType.DMA
    return pl.pallas_call(
        bound(step_kernel, sizes),
        name="step",
        out_shape=(
            jax.ShapeDtypeStruct(fraction.shape, f32),
            jax.ShapeDtypeStruct((1,), f32),
            jax.ShapeDtypeStruct((1,), f32),
        ),
        in_specs=[smem] * 7 + [vmem] * 4,
        out_specs=(vmem, smem, smem),
        scratch_shapes=[
            pltpu.VMEM((slots, 5, 1, atoms), f32),
            pltpu.VMEM((8, 2 * mig), f32),
            pltpu.VMEM((2, 8, 2 * mig), f32),
            pltpu.VMEM((blocks, 7, LANES, LANES), f32),
            pltpu.VMEM((blocks, 3, LANES, LANES), f32),
            pltpu.VMEM((slots * blocks, 8, LANES), f32),
            pltpu.VMEM((3, 8, LANES), f32),
            pltpu.VMEM((8, LANES), f32),
            pltpu.VMEM((total, 8, LANES), f32),
            dma((2,)),
            dma((2,)),
            dma((slots,)),
            dma((slots,)),
            dma((total,)),
            dma((total,)),
        ],
        compiler_params=pltpu.CompilerParams(collective_id=0, has_side_effects=True),
    )(
        domain_edge,
        coupling,
        sigma_table,
        depth_table,
        charge_table,
        neighbours.reshape(blocks, 1, -1),
        counts,
        fraction,
        atom_type,
        perturbed,
        leaving,
    )


def solution(mesh):
    sizes = (mesh.shape["dx"], mesh.shape["dy"], mesh.shape["dz"])
    return jax.shard_map(
        lambda *arrays: on_device(sizes, *arrays),
        mesh=mesh,
        in_specs=(
            P(None, ("win", "dx"), "dy", "dz", None),
            P(("win", "dx"), "dy", "dz", None),
            P(("win", "dx"), "dy", "dz", None),
            P(("win", "dx"), "dy", "dz", None, None),
            P(("win", "dx"), "dy", "dz", None, None),
            P(("win", "dx"), "dy", "dz", None),
            P(),
            P(),
            P(),
            P(),
            P("win"),
        ),
        out_specs=(P(None, ("win", "dx"), "dy", "dz", None), P("win"), P("win")),
        check_vma=False,
    )
```

profile of v0, /device:TPU:0, one launch (start us, length us, event | category | flops | bytes accessed | tf_op | source)
XLA Modules:
  0.0 39.5 jit_solution(9392003931020881873)
XLA Ops:
  1.3 33.4 %step.1 = (f32[3,1,1,1,768]{4,3,2,1,0:T(1,128)}, f32[1]{0:T(128)}, f32[1]{0:T(128)}) custom-call(f32[3]{0:T(128)} %refs_0_.1, f32[1]{0:T(128)S(6)} %copy.17.refs_1_, f32[32]{0:T(128)} %refs_2_.1, f32[32]{0:T(128)} %refs_3_.1, f32[32]{0:T(128)} %refs_4_.1, s32[6,1,16]{2,1,0:T(1,128)} %bitcast.1, s32[1,1,1,6]{3,2,1,0:T(1,128)} %refs_6_.1, ...), custom_call_target="tpu_custom_call" | custom-call | tf_op jit(solution)/shard_map/step/pallas_call | solution.py:364
  34.7 1.3 %copy.18 = f32[3,1,1,1,768]{4,3,2,1,0:T(1,128)} copy(f32[3,1,1,1,768]{4,3,2,1,0:T(1,128)} %get-tuple-element.6) | data formatting | bytes 18432
where the time goes:
time: 39.7 us; the launch traced here: 39.5 us
  Pallas kernels  33.4 us (84%)
  between operations  4.81 us (12%)
  local copies, waits for them, and re-layouts  1.3 us (3%)
    pallas_call x1, Pallas kernels, on_device(): pl.pallas_call(bound(step_kernel, sizes), name='step', out_shape=(jax.Sha...  33.4 us
    unnamed x1, local copies, waits for them, and re-layouts  1.3 us

commit v1 on v0

--- a/solution.py
+++ b/solution.py
@@ -40,36 +40,41 @@
 
 def step_kernel(
     sizes,
-    edge_ref,
-    coupling_ref,
-    sigma_ref,
-    depth_ref,
-    charge_ref,
-    listed_ref,
-    count_ref,
-    fraction_ref,
-    type_ref,
-    flag_ref,
-    leaving_ref,
-    force_ref,
-    energy_ref,
-    dhdl_ref,
-    ghost_ref,
-    outgoing,
-    incoming,
-    own_cols,
-    force_acc,
-    params,
-    sums_ref,
-    tile,
-    gathered,
-    mig_send,
-    mig_recv,
-    send_sem,
-    recv_sem,
-    sum_send,
-    sum_recv,
+    *refs,
 ):
+    inputs, refs = refs[:11], refs[11:]
+    force_ref, tally_ref, *refs = refs
+    staged, (load_sem, *refs) = refs[:11], refs[11:]
+    (
+        edge_ref,
+        coupling_ref,
+        sigma_ref,
+        depth_ref,
+        charge_ref,
+        listed_ref,
+        count_ref,
+        fraction_ref,
+        type_ref,
+        flag_ref,
+        leaving_ref,
+    ) = staged
+    (
+        ghost_ref,
+        outgoing,
+        incoming,
+        own_cols,
+        force_acc,
+        params,
+        sums_ref,
+        tile,
+        gathered,
+        mig_send,
+        mig_recv,
+        send_sem,
+        recv_sem,
+        sum_send,
+        sum_recv,
+    ) = refs
     nx, ny, nz = sizes
     atoms = fraction_ref.shape[-1]
     spacing = float(atoms) ** (1.0 / 3.0)
@@ -108,6 +113,15 @@
             device_id=window_device(lax.rem(my_id + by, total)),
             device_id_type=MESH,
         )
+
+    loads = [
+        pltpu.make_async_copy(source, target, load_sem.at[k])
+        for k, (source, target) in enumerate(zip(inputs, staged))
+    ]
+    for load in loads:
+        load.start()
+    for load in loads:
+        load.wait()
 
     own = ghost_ref.at[slot((0, 0, 0))]
     edge = [edge_ref[k] * spacing for k in range(3)]
@@ -341,8 +355,18 @@
     summed = jnp.sum(gathered[...], axis=0)
     parts = [jnp.sum(summed[k : k + 1]) for k in range(3)]
     scale = 0.5 / float(atoms * total)
-    energy_ref[0] = scale * (parts[0] - lam * parts[1])
-    dhdl_ref[0] = -scale * (parts[1] + (0.5 * (1.0 - lam)) * parts[2])
+    rows = lax.broadcasted_iota(jnp.int32, (8, LANES), 0)
+    energy = scale * (parts[0] - lam * parts[1])
+    dhdl = -scale * (parts[1] + (0.5 * (1.0 - lam)) * parts[2])
+    tally_ref[...] = jnp.where(rows == 0, energy, dhdl)
+
+
+def hand_over(force_in, tally_in, force_ref, energy_ref, dhdl_ref, sem):
+    copy = pltpu.make_async_copy(force_in, force_ref, sem)
+    copy.start()
+    energy_ref[0] = tally_in[0, 0]
+    dhdl_ref[0] = tally_in[1, 0]
+    copy.wait()
 
 
 def on_device(sizes, fraction, atom_type, perturbed, leaving, neighbours, counts,
@@ -361,17 +385,29 @@
     blocks = atoms // LANES
     total = nx * ny * nz
     dma = pltpu.SemaphoreType.DMA
-    return pl.pallas_call(
+    arrays = (
+        domain_edge,
+        coupling,
+        sigma_table,
+        depth_table,
+        charge_table,
+        neighbours.reshape(blocks, 1, -1),
+        counts,
+        fraction,
+        atom_type,
+        perturbed,
+        leaving,
+    )
+    forces, tally = pl.pallas_call(
         bound(step_kernel, sizes),
         name="step",
-        out_shape=(
-            jax.ShapeDtypeStruct(fraction.shape, f32),
-            jax.ShapeDtypeStruct((1,), f32),
-            jax.ShapeDtypeStruct((1,), f32),
-        ),
-        in_specs=[smem] * 7 + [vmem] * 4,
-        out_specs=(vmem, smem, smem),
+        out_shape=(pltpu.VMEM(fraction.shape, f32), pltpu.VMEM((8, LANES), f32)),
+        in_specs=[pl.BlockSpec(memory_space=pl.ANY)] * 11,
+        out_specs=(vmem, vmem),
         scratch_shapes=[
+            *(pltpu.SMEM(x.shape, x.dtype) for x in arrays[:7]),
+            *(pltpu.VMEM(x.shape, x.dtype) for x in arrays[7:]),
+            dma((11,)),
             pltpu.VMEM((slots, 5, 1, atoms), f32),
             pltpu.VMEM((8, 2 * mig), f32),
             pltpu.VMEM((2, 8, 2 * mig), f32),
@@ -389,19 +425,19 @@
             dma((total,)),
         ],
         compiler_params=pltpu.CompilerParams(collective_id=0, has_side_effects=True),
-    )(
-        domain_edge,
-        coupling,
-        sigma_table,
-        depth_table,
-        charge_table,
-        neighbours.reshape(blocks, 1, -1),
-        counts,
-        fraction,
-        atom_type,
-        perturbed,
-        leaving,
-    )
+    )(*arrays)
+    return pl.pallas_call(
+        hand_over,
+        name="hand_over",
+        out_shape=(
+            jax.ShapeDtypeStruct(fraction.shape, f32),
+            jax.ShapeDtypeStruct((1,), f32),
+            jax.ShapeDtypeStruct((1,), f32),
+        ),
+        in_specs=[vmem, vmem],
+        out_specs=(pl.BlockSpec(memory_space=pl.ANY), smem, smem),
+        scratch_shapes=[pltpu.SemaphoreType.DMA],
+    )(pltpu.with_memory_space_constraint(forces, pltpu.VMEM), pltpu.with_memory_space_constraint(tally, pltpu.VMEM))
 
 
 def solution(mesh):

time: 39.7 us -> 34.7 us (0.87)
  between operations: 4.81 us -> 1.29 us
  local copies, waits for them, and re-layouts: 1.3 us -> 0 us
    unnamed x1 -> x0, local copies, waits for them, and re-layouts: 1.3 us -> none
    pallas_call x1 -> x2, Pallas kernels: 33.4 us -> 33.2 us  [the longest x1 32.1 us: on_device(): pl.pallas_call(bound(step_kernel, sizes), name='step', out_shape=(pltpu.V...]
where the time goes in v1:
time: 34.7 us; the launch traced here: 34.5 us
  Pallas kernels  33.2 us (96%)
  between operations  1.29 us (4%)
    pallas_call x1, Pallas kernels, on_device(): pl.pallas_call(bound(step_kernel, sizes), name='step', out_shape=(pltpu.V...  32.1 us
    pallas_call x1, Pallas kernels, on_device(): pl.pallas_call(hand_over, name='hand_over', out_shape=(jax.ShapeDtypeStru...  1.13 us

profile of v1, /device:TPU:0, one launch (start us, length us, event | category | flops | bytes accessed | tf_op | source)
XLA Modules:
  0.0 34.5 jit_solution(3243145328243576972)
XLA Ops:
  1.3 32.1 %step.1 = (f32[3,1,1,1,768]{4,3,2,1,0:T(1,128)S(1)}, f32[8,128]{1,0:T(8,128)S(1)}) custom-call(f32[3]{0:T(128)} %refs_0_.1, f32[1]{0:T(128)S(6)} %copy.14.refs_1_, f32[32]{0:T(128)} %refs_2_.1, f32[32]{0:T(128)} %refs_3_.1, f32[32]{0:T(128)} %refs_4_.1, s32[6,1,16]{2,1,0:T(1,128)} %bitcast.1, s32[1,1,1,6]{3,2,1,0:T(1,128)} %refs_6_.1, ...), custom_call_target="tpu_custom_call" | custom-call | tf_op jit(solution)/shard_map/step/pallas_call | solution.py:401
  33.4 1.1 %hand_over.1 = (f32[3,1,1,1,768]{4,3,2,1,0:T(1,128)}, f32[1]{0:T(128)}, f32[1]{0:T(128)}) custom-call(f32[3,1,1,1,768]{4,3,2,1,0:T(1,128)S(1)} %get-tuple-element.5.force_in, f32[8,128]{1,0:T(8,128)S(1)} %get-tuple-element.6.tally_in), custom_call_target="tpu_custom_call" | custom-call | tf_op jit(solution)/shard_map/hand_over/pallas_call | solution.py:429

commit v2 on v1

--- a/solution.py
+++ b/solution.py
@@ -12,7 +12,8 @@
 coulomb = 0.1
 LANES = 128
 MESH = pl.DeviceIdType.MESH
-HIGHEST = lax.Precision.HIGHEST
+ROWS = 5
+FORMS = 6
 
 
 def steps_of(count):
@@ -27,11 +28,19 @@
     return step + 1
 
 
-def thirds(value):
+def split(value):
     high = value.astype(jnp.bfloat16).astype(jnp.float32)
     rest = value - high
     middle = rest.astype(jnp.bfloat16).astype(jnp.float32)
-    return jnp.concatenate([high, middle, rest - middle], axis=0)
+    return high, middle, rest - middle
+
+
+def thirds(value):
+    return jnp.concatenate(split(value), axis=0)
+
+
+def onehot(hits):
+    return hits.astype(jnp.float32).astype(jnp.bfloat16)
 
 
 def joined(value):
@@ -48,11 +57,11 @@
     (
         edge_ref,
         coupling_ref,
+        listed_ref,
+        count_ref,
         sigma_ref,
         depth_ref,
         charge_ref,
-        listed_ref,
-        count_ref,
         fraction_ref,
         type_ref,
         flag_ref,
@@ -64,7 +73,11 @@
         incoming,
         own_cols,
         force_acc,
-        params,
+        table_ref,
+        lhs_ref,
+        self_ref,
+        forms_a,
+        forms_b,
         sums_ref,
         tile,
         gathered,
@@ -77,6 +90,9 @@
     ) = refs
     nx, ny, nz = sizes
     atoms = fraction_ref.shape[-1]
+    blocks = atoms // LANES
+    width = listed_ref.shape[-1]
+    kinds = sigma_ref.shape[-1]
     spacing = float(atoms) ** (1.0 / 3.0)
     me = (lax.axis_index("dx"), lax.axis_index("dy"), lax.axis_index("dz"))
 
@@ -124,8 +140,8 @@
         load.wait()
 
     own = ghost_ref.at[slot((0, 0, 0))]
-    edge = [edge_ref[k] * spacing for k in range(3)]
-    rows = [fraction_ref[k, 0, 0] * edge[k] for k in range(3)]
+    edge = [edge_ref[k] * (spacing * 3.0**-0.5) for k in range(3)]
+    rows = [(fraction_ref[k, 0, 0] - 0.5) * edge[k] for k in range(3)]
     rows += [type_ref[0, 0].astype(jnp.float32), flag_ref[0, 0].astype(jnp.float32)]
     payload = jnp.concatenate(rows + [jnp.zeros((3, atoms), jnp.float32)], axis=0)
     leave = leaving_ref[0, 0, 0]
@@ -170,8 +186,9 @@
         move.wait()
     merged = jnp.where(lane < mig, incoming[1], incoming[0])
     moved = jnp.where(gone > 0.5, joined(spread(thirds(merged))), payload)
-    for r in range(5):
-        own[r] = moved[r : r + 1]
+    for q in range(blocks):
+        for r in range(ROWS):
+            own[q, r] = moved[r : r + 1, q * LANES : (q + 1) * LANES]
     copies = []
     for k, o in enumerate(sorted(others, key=lambda o: -sum(map(abs, o)))):
         copy = pltpu.make_async_remote_copy(
@@ -185,138 +202,231 @@
         copy.start()
         copies.append((copy, slot(o)))
 
-    blocks = atoms // LANES
     lam = coupling_ref[0]
     own_slot = slot((0, 0, 0))
     ones = jnp.ones((8, LANES), jnp.bfloat16)
-    for k in range(3):
+    for k in range(2):
         sums_ref[k] = jnp.zeros((8, LANES), jnp.float32)
 
-    ahead = lax.broadcasted_iota(jnp.int32, (8, LANES), 1) - lax.broadcasted_iota(
-        jnp.int32, (8, LANES), 0
+    pairs = 2 * kinds
+    flat = lax.broadcasted_iota(jnp.int32, (1, LANES), 1)
+
+    def per_kind(ref):
+        row = ref[...]
+        return jnp.concatenate([row] * (LANES // kinds), axis=1)
+
+    halved = per_kind(sigma_ref) * 0.5
+    depth = jnp.sqrt(per_kind(depth_ref)) * 2.0
+    charge = per_kind(charge_ref)
+    flag = jnp.where(lax.rem(flat, pairs) < kinds, 0.0, 1.0)
+    stack = jnp.concatenate(
+        [halved, depth, charge, flag, jnp.zeros((4, LANES), jnp.float32)], axis=0
+    ).T
+
+    def column(k):
+        return jnp.broadcast_to(stack[:pairs, k : k + 1], (pairs, LANES))
+
+    six = column(0) + halved
+    six = six * six
+    six = six * six * six * (1.0 / 27.0)
+    either = jnp.maximum(column(3), flag)
+    soft = soft_base + (soft_alpha * lam) * either
+    weight = 1.0 - lam * either
+    root2 = 2.0**0.5
+    tables = [
+        2.0 * soft,
+        six,
+        six * soft,
+        column(1) * depth * weight,
+        (column(2) * (coulomb * root2)) * charge * weight,
+    ]
+    low_half = lax.broadcasted_iota(jnp.int32, (pairs, LANES), 1) < pairs
+    for f, whole in enumerate(tables):
+        high, middle, low = split(whole)
+        for half, part in enumerate(
+            (jnp.where(low_half, high, middle), jnp.where(low_half, low, 0.0))
+        ):
+            at = (2 * f + half) * LANES
+            table_ref[:, at : at + LANES] = jnp.concatenate(
+                [part, jnp.zeros((LANES - pairs, LANES), jnp.float32)], axis=0
+            ).astype(jnp.bfloat16)
+
+    scaled = 2.0 / (1.0 - lam)
+    soft = soft_base + (soft_alpha * lam) * flag
+    weight = 1.0 - lam * flag
+    root = lax.rsqrt(2.0 * soft)
+    ratio = 1.0 / soft
+    electric = (coulomb * root2) * charge * charge * weight * root
+    strength = depth * depth * weight * ratio
+    alone = strength * (ratio - 1.0) + electric
+    slope = strength * (ratio + (ratio - 1.0)) * ratio + electric * (root * root)
+    both = jnp.concatenate(
+        [alone, flag * (scaled * alone + slope), jnp.zeros((6, LANES), jnp.float32)], axis=0
     )
-    lane = lax.broadcasted_iota(jnp.int32, (1, LANES), 1)
-    tables = [jnp.zeros((1, LANES), jnp.float32)] * 3
-    for k in range(sigma_ref.shape[0]):
-        hit = lane == k
-        tables = [
-            jnp.where(hit, ref[k], table)
-            for ref, table in zip((sigma_ref, depth_ref, charge_ref), tables)
-        ]
-    table = jnp.concatenate(
-        [tables[0] * 0.5, jnp.sqrt(tables[1]) * 2.0, tables[2]] + [tables[2] * 0.0] * 5, axis=0
+    self_parts = thirds(both[:, :pairs]).astype(jnp.bfloat16)
+
+    kind_rows = lax.broadcasted_iota(jnp.int32, (pairs, LANES), 0).astype(jnp.float32)
+    kind_lane = lax.broadcasted_iota(jnp.int32, (LANES, LANES), 1).astype(jnp.float32)
+    deep = lax.broadcasted_iota(jnp.int32, (8, LANES), 0)
+    unit3 = jnp.where(deep == 3, 1.0, 0.0)
+    picks = onehot(
+        lax.broadcasted_iota(jnp.int32, (24, ROWS * LANES), 0) % 8
+        == lax.broadcasted_iota(jnp.int32, (24, ROWS * LANES), 1) // LANES
     )
-    kinds = sigma_ref.shape[0]
-    table_parts = thirds(table[:, :kinds]).astype(jnp.bfloat16)
-    kind_row = lax.broadcasted_iota(jnp.int32, (kinds, atoms), 0).astype(jnp.float32)
-
-    def look_up(place):
-        onehot = (kind_row == ghost_ref[place, 3]).astype(jnp.float32).astype(jnp.bfloat16)
-        found = joined(jnp.dot(table_parts, onehot, preferred_element_type=jnp.float32))
-        rows = [ghost_ref[place, r] for r in range(3)]
-        rows += [found[0:3], ghost_ref[place, 4], found[3:4]]
-        whole = jnp.concatenate(rows, axis=0)
-        for q in range(blocks):
-            params[place * blocks + q] = whole[:, q * LANES : (q + 1) * LANES]
-
-    look_up(own_slot)
-    picks = (
-        lax.broadcasted_iota(jnp.int32, (24, 7 * LANES), 0) % 8
-        == lax.broadcasted_iota(jnp.int32, (24, 7 * LANES), 1) // LANES
-    ).astype(jnp.float32).astype(jnp.bfloat16)
-    for q in range(blocks):
-        cols = thirds(params[own_slot * blocks + q]).T.astype(jnp.bfloat16)
-        wide = jnp.dot(cols, picks, preferred_element_type=jnp.float32)
-        for r in range(7):
-            col = wide[:, r * LANES : (r + 1) * LANES]
-            own_cols[q, r] = col * coulomb if r == 5 else col
-    for q in range(blocks):
+
+    def kind_of(place, block):
+        return ghost_ref[place, block, 3] + float(kinds) * ghost_ref[place, block, 4]
+
+    @pl.loop(0, blocks)
+    def _(q):
+        kind = kind_of(own_slot, q)
+        xyz = [ghost_ref[own_slot, q, r] for r in range(3)]
+        blank = jnp.zeros((1, LANES), jnp.float32)
+        rows = jnp.concatenate(
+            xyz + [ghost_ref[own_slot, q, 4], kind, blank, blank, blank], axis=0
+        )
+        wide = jnp.dot(
+            thirds(rows).T.astype(jnp.bfloat16), picks, preferred_element_type=jnp.float32
+        )
+        for r in range(4):
+            own_cols[q, r] = wide[:, r * LANES : (r + 1) * LANES]
+        norm = xyz[0] * xyz[0] + xyz[1] * xyz[1] + xyz[2] * xyz[2]
+        base = jnp.concatenate(
+            [x * -2.0 for x in xyz] + [blank, norm, blank, blank, blank], axis=0
+        )
+        geo = []
+        for factor in (1.0, 6.0):
+            high, middle, low = split(base * factor)
+            unit = unit3 * factor
+            groups = [high + unit, middle, low, high + unit, middle, high + unit]
+            above = jnp.zeros((pairs, LANES), jnp.float32)
+            below = jnp.zeros((LANES - pairs - 48, LANES), jnp.float32)
+            geo.append(jnp.concatenate([above] + groups + [below], axis=0).T)
+        hot = onehot(wide[:, 4 * LANES : 5 * LANES] == kind_lane)
+        looked = jnp.dot(hot, table_ref[...], preferred_element_type=jnp.float32)
+        lhs_ref[q, 0:LANES, 0:LANES] = jnp.zeros((LANES, LANES), jnp.bfloat16)
+        lhs_ref[q, 0:LANES, LANES : 2 * LANES] = geo[0].astype(jnp.bfloat16)
+        for f in range(FORMS - 1):
+            left = looked[:, 2 * f * LANES : (2 * f + 1) * LANES]
+            right = looked[:, (2 * f + 1) * LANES : (2 * f + 2) * LANES]
+            if f == 0:
+                right = right + geo[1]
+            at = slice((f + 1) * LANES, (f + 2) * LANES)
+            lhs_ref[q, at, 0:LANES] = left.astype(jnp.bfloat16)
+            lhs_ref[q, at, LANES : 2 * LANES] = right.astype(jnp.bfloat16)
+        mine = joined(
+            jnp.dot(self_parts, onehot(kind_rows == kind), preferred_element_type=jnp.float32)
+        )
+        for k in range(2):
+            self_ref[q, k] = jnp.where(deep == 0, mine[k : k + 1], 0.0)
         for k in range(3):
             force_acc[q, k] = jnp.zeros((LANES, LANES), jnp.float32)
 
     for copy, place in copies:
         copy.wait()
-        look_up(place)
-
-    @pl.loop(0, blocks)
-    def _(q):
-        def entry(e):
-            listed = listed_ref[q, 0, e]
-            left = jnp.minimum(jnp.maximum(count_ref[0, 0, 0, q] - e, 0), 1)
-            used = left.astype(jnp.float32)
-            apart = jnp.abs(listed - (13 * blocks + q))
-            self_lane = jnp.minimum(apart, 1) * (2 * LANES)
-            image = lax.div(listed, blocks)
-            a = lax.div(image, 9) - 1
-            b = lax.rem(lax.div(image, 3), 3) - 1
-            c = lax.rem(image, 3) - 1
-            where_from = (
-                slot_step(a, nx) * len(steps_of(ny)) + slot_step(b, ny)
-            ) * len(steps_of(nz)) + slot_step(c, nz)
-            other = params[where_from * blocks + lax.rem(listed, blocks)]
-            rows = []
-            for r in range(7):
-                row = other[r : r + 1]
-                if r < 3:
-                    row = row + (a, b, c)[r].astype(jnp.float32) * edge[r]
-                if 4 <= r < 6:
-                    row = row * used
-                rows.append(jnp.broadcast_to(row, (8, LANES)))
-            xj, yj, zj, hj, ej, qj, pj = rows
-
-            tot = jnp.zeros((8, LANES), jnp.float32)
-            tot_p = jnp.zeros((8, LANES), jnp.float32)
-            tot_k = jnp.zeros((8, LANES), jnp.float32)
-            for g in range(LANES // 8):
-                at = pl.ds(g * 8, 8)
-                dx = own_cols[q, 0, at] - xj
-                dy = own_cols[q, 1, at] - yj
-                dz = own_cols[q, 2, at] - zj
-                r2 = dx * dx + dy * dy + dz * dz
-                sig = own_cols[q, 3, at] + hj
-                s2 = sig * sig
-                s6 = s2 * s2 * s2
-                eps4 = own_cols[q, 4, at] * ej
-                qq = own_cols[q, 5, at] * qj
-                diag = ahead == self_lane + g * 8
-                eps4 = jnp.where(diag, 0.0, eps4)
-                qq = jnp.where(diag, 0.0, qq)
-                p = jnp.maximum(own_cols[q, 6, at], pj)
-                soft = soft_base + (soft_alpha * lam) * p
-                weight = 1.0 - lam * p
+
+    def entry(q, e):
+        listed = listed_ref[q, 0, e]
+        left = jnp.minimum(jnp.maximum(count_ref[0, 0, 0, q] - e, 0), 1)
+        apart = jnp.abs(listed - (13 * blocks + q))
+        image = lax.div(listed, blocks)
+        step = (
+            lax.div(image, 9) - 1,
+            lax.rem(lax.div(image, 3), 3) - 1,
+            lax.rem(image, 3) - 1,
+        )
+        where_from = (
+            slot_step(step[0], nx) * len(steps_of(ny)) + slot_step(step[1], ny)
+        ) * len(steps_of(nz)) + slot_step(step[2], nz)
+        block = lax.rem(listed, blocks)
+        away = (1 - left).astype(jnp.float32) * 1024.0
+        by = [step[k].astype(jnp.float32) * edge[k] for k in range(3)]
+        by[0] = by[0] + away
+        xyz = [ghost_ref[where_from, block, r] + by[r] for r in range(3)]
+        itself = ((1 - jnp.minimum(apart, 1)) * left).astype(jnp.float32)
+        return where_from, block, xyz, left, itself
+
+    def features(q, e):
+        place, block, xyz, left, _ = entry(q, e)
+        norm = xyz[0] * xyz[0] + xyz[1] * xyz[1] + xyz[2] * xyz[2]
+        blank = jnp.zeros((1, LANES), jnp.float32)
+        rows = jnp.concatenate(xyz + [norm, blank + 1.0, blank, blank, blank], axis=0)
+        high, middle, low = split(rows)
+        kind = kind_of(place, block) - (1 - left).astype(jnp.float32) * float(2 * pairs)
+        hot = onehot(kind_rows == kind)
+        near = jnp.concatenate([high, high, high, middle, middle, low], axis=0)
+        near = jnp.concatenate(
+            [near, jnp.zeros((2 * LANES - 3 * pairs - 48, LANES), jnp.float32)], axis=0
+        ).astype(jnp.bfloat16)
+        return jnp.concatenate([hot, hot, hot, near], axis=0)
+
+    per_block = width // 2
+
+    def produce(t, forms):
+        q = lax.div(t, per_block)
+        e = 2 * lax.rem(t, per_block)
+        rhs = jnp.concatenate([features(q, e), features(q, e + 1)], axis=1)
+        forms[...] = jnp.dot(lhs_ref[q], rhs, preferred_element_type=jnp.float32)
+
+    def consume(t, forms):
+        q = lax.div(t, per_block)
+        e = 2 * lax.rem(t, per_block)
+        others = []
+        tot = jnp.zeros((8, LANES), jnp.float32)
+        tot_p = jnp.zeros((8, LANES), jnp.float32)
+        for k in range(2):
+            place, block, xyz, _, itself = entry(q, e + k)
+            others.append(
+                [
+                    jnp.broadcast_to(row, (8, LANES))
+                    for row in xyz + [ghost_ref[place, block, 4]]
+                ]
+            )
+            tot = tot - itself * self_ref[q, 0]
+            tot_p = tot_p - itself * self_ref[q, 1]
+        for g in range(LANES // 8):
+            at = pl.ds(g * 8, 8)
+            xi, yi, zi, pi = (own_cols[q, r, at] for r in range(4))
+            fx = fy = fz = None
+            for k, (xj, yj, zj, pj) in enumerate(others):
+                r2, s2, s6, soft6, eps, qq = (
+                    forms[f * LANES + g * 8 : f * LANES + g * 8 + 8, k * LANES : (k + 1) * LANES]
+                    for f in range(FORMS)
+                )
                 r4 = r2 * r2
-                soft6 = s6 * soft + r4 * r2
-                inv = 1.0 / soft6
-                u = lax.rsqrt(soft + r2)
+                inv = 1.0 / (soft6 + r4 * r2)
+                u = lax.rsqrt(s2)
                 ec = qq * u
-                half = (0.5 * ec) * (u * u)
-                t = s6 * inv
-                et = eps4 * t
-                tm = t - 1.0
+                half = ec * (u * u)
+                t6 = s6 * inv
+                et = eps * t6
+                tm = t6 - 1.0
                 v = et * tm + ec
-                m = et * (t + tm)
-                kk = m * t + half
-                fs = weight * (3.0 * (m * (r4 * inv)) + half)
+                m = et * (t6 + tm)
+                kk = m * t6 + half
+                fs = m * (r4 * inv) + half
                 tot = tot + v
-                tot_p = tot_p + p * v
-                tot_k = tot_k + p * kk
-                force_acc[q, 0, at] += fs * dx
-                force_acc[q, 1, at] += fs * dy
-                force_acc[q, 2, at] += fs * dz
-            sums_ref[0] += tot
-            sums_ref[1] += tot_p
-            sums_ref[2] += tot_k
-
-        width = listed_ref.shape[-1]
-        unroll = 4 if width % 4 == 0 else 1
-
-        @pl.loop(0, width // unroll)
-        def _(step):
-            for k in range(unroll):
-                entry(step * unroll + k)
-
-    folded = [jnp.sum(sums_ref[k], axis=0, keepdims=True) for k in range(3)]
-    folded.append(jnp.zeros((5, LANES), jnp.float32))
+                tot_p = tot_p + jnp.maximum(pi, pj) * (scaled * v + kk)
+                gx, gy, gz = fs * (xi - xj), fs * (yi - yj), fs * (zi - zj)
+                fx, fy, fz = (gx, gy, gz) if fx is None else (fx + gx, fy + gy, fz + gz)
+            force_acc[q, 0, at] += fx
+            force_acc[q, 1, at] += fy
+            force_acc[q, 2, at] += fz
+        sums_ref[0] += tot
+        sums_ref[1] += tot_p
+
+    steps = blocks * per_block
+    produce(0, forms_a)
+
+    @pl.loop(0, steps // 2)
+    def _(s):
+        produce(2 * s + 1, forms_b)
+        consume(2 * s, forms_a)
+        produce(jnp.minimum(2 * s + 2, steps - 1), forms_a)
+        consume(2 * s + 1, forms_b)
+
+    folded = [jnp.sum(sums_ref[k], axis=0, keepdims=True) for k in range(2)]
+    folded.append(jnp.zeros((6, LANES), jnp.float32))
     mine = jnp.concatenate(folded, axis=0)
     tile[...] = mine
     gathered[my_id] = mine
@@ -346,18 +456,18 @@
                 )
                 for part in (high, low)
             )
-            force_ref[k, 0, 0, :, q * LANES : (q + 1) * LANES] = 2.0 * reduced[0:1]
+            force_ref[k, 0, 0, :, q * LANES : (q + 1) * LANES] = (2.0 * 3.0**0.5) * reduced[0:1]
 
     @pl.loop(1, total)
     def _(by):
         share(by).wait()
 
     summed = jnp.sum(gathered[...], axis=0)
-    parts = [jnp.sum(summed[k : k + 1]) for k in range(3)]
+    parts = [jnp.sum(summed[k : k + 1]) for k in range(2)]
     scale = 0.5 / float(atoms * total)
     rows = lax.broadcasted_iota(jnp.int32, (8, LANES), 0)
-    energy = scale * (parts[0] - lam * parts[1])
-    dhdl = -scale * (parts[1] + (0.5 * (1.0 - lam)) * parts[2])
+    energy = scale * parts[0]
+    dhdl = (-0.5 * scale) * parts[1]
     tally_ref[...] = jnp.where(rows == 0, energy, dhdl)
 
 
@@ -388,11 +498,9 @@
     arrays = (
         domain_edge,
         coupling,
-        sigma_table,
-        depth_table,
-        charge_table,
         neighbours.reshape(blocks, 1, -1),
         counts,
+        *(table.reshape(1, -1) for table in (sigma_table, depth_table, charge_table)),
         fraction,
         atom_type,
         perturbed,
@@ -405,16 +513,20 @@
         in_specs=[pl.BlockSpec(memory_space=pl.ANY)] * 11,
         out_specs=(vmem, vmem),
         scratch_shapes=[
-            *(pltpu.SMEM(x.shape, x.dtype) for x in arrays[:7]),
-            *(pltpu.VMEM(x.shape, x.dtype) for x in arrays[7:]),
+            *(pltpu.SMEM(x.shape, x.dtype) for x in arrays[:4]),
+            *(pltpu.VMEM(x.shape, x.dtype) for x in arrays[4:]),
             dma((11,)),
-            pltpu.VMEM((slots, 5, 1, atoms), f32),
+            pltpu.VMEM((slots, blocks, ROWS, 1, LANES), f32),
             pltpu.VMEM((8, 2 * mig), f32),
             pltpu.VMEM((2, 8, 2 * mig), f32),
-            pltpu.VMEM((blocks, 7, LANES, LANES), f32),
+            pltpu.VMEM((blocks, 4, LANES, LANES), f32),
             pltpu.VMEM((blocks, 3, LANES, LANES), f32),
-            pltpu.VMEM((slots * blocks, 8, LANES), f32),
-            pltpu.VMEM((3, 8, LANES), f32),
+            pltpu.VMEM((LANES, 2 * (FORMS - 1) * LANES), jnp.bfloat16),
+            pltpu.VMEM((blocks, FORMS * LANES, 2 * LANES), jnp.bfloat16),
+            pltpu.VMEM((blocks, 2, 8, LANES), f32),
+            pltpu.VMEM((FORMS * LANES, 2 * LANES), f32),
+            pltpu.VMEM((FORMS * LANES, 2 * LANES), f32),
+            pltpu.VMEM((2, 8, LANES), f32),
             pltpu.VMEM((8, LANES), f32),
             pltpu.VMEM((total, 8, LANES), f32),
             dma((2,)),

time: 34.7 us -> 37.2 us (1.072)
  Pallas kernels: 33.2 us -> 35.7 us
    pallas_call x1, Pallas kernels: 32.1 us -> 34.6 us  [on_device(): pl.pallas_call(bound(step_kernel, sizes), name='step', out_shape=(pltpu.V...]
where the time goes in v2:
time: 37.2 us; the launch traced here: 37 us
  Pallas kernels  35.7 us (96%)
  between operations  1.29 us (3%)
    pallas_call x1, Pallas kernels, on_device(): pl.pallas_call(bound(step_kernel, sizes), name='step', out_shape=(pltpu.V...  34.6 us
    pallas_call x1, Pallas kernels, on_device(): pl.pallas_call(hand_over, name='hand_over', out_shape=(jax.ShapeDtypeStru...  1.13 us

profile of v2, /device:TPU:0, one launch (start us, length us, event | category | flops | bytes accessed | tf_op | source)
XLA Modules:
  0.0 37.0 jit_solution(17127141225164133990)
XLA Ops:
  1.3 34.6 %step.1 = (f32[3,1,1,1,768]{4,3,2,1,0:T(1,128)S(1)}, f32[8,128]{1,0:T(8,128)S(1)}) custom-call(f32[3]{0:T(128)} %refs_0_.1, f32[1]{0:T(128)S(6)} %copy.14.refs_1_, s32[6,1,16]{2,1,0:T(1,128)} %bitcast.4, s32[1,1,1,6]{3,2,1,0:T(1,128)} %refs_3_.1, f32[1,32]{1,0:T(1,128)} %bitcast.5, f32[1,32]{1,0:T(1,128)} %bitcast.6, f32[1,32]{1,0:T(1,128)} %bitcast.7, ...), custom_call_target="tpu_custom_call" | custom-call | tf_op jit(solution)/shard_map/step/pallas_call | solution.py:509
  35.9 1.1 %hand_over.1 = (f32[3,1,1,1,768]{4,3,2,1,0:T(1,128)}, f32[1]{0:T(128)}, f32[1]{0:T(128)}) custom-call(f32[3,1,1,1,768]{4,3,2,1,0:T(1,128)S(1)} %get-tuple-element.5.force_in, f32[8,128]{1,0:T(8,128)S(1)} %get-tuple-element.6.tally_in), custom_call_target="tpu_custom_call" | custom-call | tf_op jit(solution)/shard_map/hand_over/pallas_call | solution.py:541

commit v3 on v1

--- a/solution.py
+++ b/solution.py
@@ -12,7 +12,7 @@
 coulomb = 0.1
 LANES = 128
 MESH = pl.DeviceIdType.MESH
-HIGHEST = lax.Precision.HIGHEST
+COLS = 9
 
 
 def steps_of(count):
@@ -65,6 +65,7 @@
         own_cols,
         force_acc,
         params,
+        self_ref,
         sums_ref,
         tile,
         gathered,
@@ -124,7 +125,7 @@
         load.wait()
 
     own = ghost_ref.at[slot((0, 0, 0))]
-    edge = [edge_ref[k] * spacing for k in range(3)]
+    edge = [edge_ref[k] * (spacing * 3.0**-0.5) for k in range(3)]
     rows = [fraction_ref[k, 0, 0] * edge[k] for k in range(3)]
     rows += [type_ref[0, 0].astype(jnp.float32), flag_ref[0, 0].astype(jnp.float32)]
     payload = jnp.concatenate(rows + [jnp.zeros((3, atoms), jnp.float32)], axis=0)
@@ -192,9 +193,6 @@
     for k in range(3):
         sums_ref[k] = jnp.zeros((8, LANES), jnp.float32)
 
-    ahead = lax.broadcasted_iota(jnp.int32, (8, LANES), 1) - lax.broadcasted_iota(
-        jnp.int32, (8, LANES), 0
-    )
     lane = lax.broadcasted_iota(jnp.int32, (1, LANES), 1)
     tables = [jnp.zeros((1, LANES), jnp.float32)] * 3
     for k in range(sigma_ref.shape[0]):
@@ -204,7 +202,9 @@
             for ref, table in zip((sigma_ref, depth_ref, charge_ref), tables)
         ]
     table = jnp.concatenate(
-        [tables[0] * 0.5, jnp.sqrt(tables[1]) * 2.0, tables[2]] + [tables[2] * 0.0] * 5, axis=0
+        [tables[0] * (0.5 * 3.0**-0.5), jnp.sqrt(tables[1]) * 2.0, tables[2]]
+        + [tables[2] * 0.0] * 5,
+        axis=0,
     )
     kinds = sigma_ref.shape[0]
     table_parts = thirds(table[:, :kinds]).astype(jnp.bfloat16)
@@ -221,15 +221,36 @@
 
     look_up(own_slot)
     picks = (
-        lax.broadcasted_iota(jnp.int32, (24, 7 * LANES), 0) % 8
-        == lax.broadcasted_iota(jnp.int32, (24, 7 * LANES), 1) // LANES
+        lax.broadcasted_iota(jnp.int32, (24, COLS * LANES), 0) % 8
+        == lax.broadcasted_iota(jnp.int32, (24, COLS * LANES), 1) // LANES
     ).astype(jnp.float32).astype(jnp.bfloat16)
+
+    def graded(flag):
+        return [soft_base + (soft_alpha * lam) * flag, 1.0 - lam * flag]
+
+    deep = lax.broadcasted_iota(jnp.int32, (8, LANES), 0)
     for q in range(blocks):
-        cols = thirds(params[own_slot * blocks + q]).T.astype(jnp.bfloat16)
+        rows = params[own_slot * blocks + q]
+        rows = jnp.concatenate([rows[0:5], rows[5:6] * (0.5 * coulomb), rows[6:8]], axis=0)
+        cols = thirds(rows).T.astype(jnp.bfloat16)
         wide = jnp.dot(cols, picks, preferred_element_type=jnp.float32)
         for r in range(7):
-            col = wide[:, r * LANES : (r + 1) * LANES]
-            own_cols[q, r] = col * coulomb if r == 5 else col
+            own_cols[q, r] = wide[:, r * LANES : (r + 1) * LANES]
+        for r, col in enumerate(graded(own_cols[q, 6])):
+            own_cols[q, 7 + r] = col
+        flag = rows[6:7]
+        (soft,) = graded(flag)[:1]
+        ratio = 1.0 / soft
+        root = lax.rsqrt(soft)
+        plain = params[own_slot * blocks + q][5:6]
+        electric = (coulomb * root) * plain * plain
+        first = rows[4:5] * rows[4:5] * ratio
+        second = first * ratio
+        alone = second - first
+        slope = (second + alone) * ratio + 0.5 * electric * (root * root)
+        alone = alone + electric
+        for k, value in enumerate((alone, flag * alone, flag * slope)):
+            self_ref[q, k] = jnp.where(deep == 0, value, 0.0)
     for q in range(blocks):
         for k in range(3):
             force_acc[q, k] = jnp.zeros((LANES, LANES), jnp.float32)
@@ -238,82 +259,82 @@
         copy.wait()
         look_up(place)
 
+    width = listed_ref.shape[-1]
+    together = 2 if width % 2 == 0 else 1
+    groups = 8 if width % (8 * together) == 0 else 1
+
+    def entry(q, e):
+        listed = listed_ref[q, 0, e]
+        left = jnp.minimum(jnp.maximum(count_ref[0, 0, 0, q] - e, 0), 1)
+        used = left.astype(jnp.float32)
+        apart = jnp.abs(listed - (13 * blocks + q))
+        itself = ((1 - jnp.minimum(apart, 1)) * left).astype(jnp.float32)
+        image = lax.div(listed, blocks)
+        a = lax.div(image, 9) - 1
+        b = lax.rem(lax.div(image, 3), 3) - 1
+        c = lax.rem(image, 3) - 1
+        where_from = (
+            slot_step(a, nx) * len(steps_of(ny)) + slot_step(b, ny)
+        ) * len(steps_of(nz)) + slot_step(c, nz)
+        other = params[where_from * blocks + lax.rem(listed, blocks)]
+        rows = []
+        for r in range(7):
+            row = other[r : r + 1]
+            if r < 3:
+                row = row + (a, b, c)[r].astype(jnp.float32) * edge[r]
+            if 4 <= r < 6:
+                row = row * used
+            rows.append(row)
+        rows += graded(rows[6])
+        return [jnp.broadcast_to(row, (8, LANES)) for row in rows], itself
+
     @pl.loop(0, blocks)
     def _(q):
-        def entry(e):
-            listed = listed_ref[q, 0, e]
-            left = jnp.minimum(jnp.maximum(count_ref[0, 0, 0, q] - e, 0), 1)
-            used = left.astype(jnp.float32)
-            apart = jnp.abs(listed - (13 * blocks + q))
-            self_lane = jnp.minimum(apart, 1) * (2 * LANES)
-            image = lax.div(listed, blocks)
-            a = lax.div(image, 9) - 1
-            b = lax.rem(lax.div(image, 3), 3) - 1
-            c = lax.rem(image, 3) - 1
-            where_from = (
-                slot_step(a, nx) * len(steps_of(ny)) + slot_step(b, ny)
-            ) * len(steps_of(nz)) + slot_step(c, nz)
-            other = params[where_from * blocks + lax.rem(listed, blocks)]
-            rows = []
-            for r in range(7):
-                row = other[r : r + 1]
-                if r < 3:
-                    row = row + (a, b, c)[r].astype(jnp.float32) * edge[r]
-                if 4 <= r < 6:
-                    row = row * used
-                rows.append(jnp.broadcast_to(row, (8, LANES)))
-            xj, yj, zj, hj, ej, qj, pj = rows
-
-            tot = jnp.zeros((8, LANES), jnp.float32)
-            tot_p = jnp.zeros((8, LANES), jnp.float32)
-            tot_k = jnp.zeros((8, LANES), jnp.float32)
+        def turn(step):
+            others = [entry(q, step * together + k) for k in range(together)]
+            tot, tot_p, tot_k = (
+                sum(-itself * self_ref[q, k] for _, itself in others) for k in range(3)
+            )
             for g in range(LANES // 8):
                 at = pl.ds(g * 8, 8)
-                dx = own_cols[q, 0, at] - xj
-                dy = own_cols[q, 1, at] - yj
-                dz = own_cols[q, 2, at] - zj
-                r2 = dx * dx + dy * dy + dz * dz
-                sig = own_cols[q, 3, at] + hj
-                s2 = sig * sig
-                s6 = s2 * s2 * s2
-                eps4 = own_cols[q, 4, at] * ej
-                qq = own_cols[q, 5, at] * qj
-                diag = ahead == self_lane + g * 8
-                eps4 = jnp.where(diag, 0.0, eps4)
-                qq = jnp.where(diag, 0.0, qq)
-                p = jnp.maximum(own_cols[q, 6, at], pj)
-                soft = soft_base + (soft_alpha * lam) * p
-                weight = 1.0 - lam * p
-                r4 = r2 * r2
-                soft6 = s6 * soft + r4 * r2
-                inv = 1.0 / soft6
-                u = lax.rsqrt(soft + r2)
-                ec = qq * u
-                half = (0.5 * ec) * (u * u)
-                t = s6 * inv
-                et = eps4 * t
-                tm = t - 1.0
-                v = et * tm + ec
-                m = et * (t + tm)
-                kk = m * t + half
-                fs = weight * (3.0 * (m * (r4 * inv)) + half)
-                tot = tot + v
-                tot_p = tot_p + p * v
-                tot_k = tot_k + p * kk
-                force_acc[q, 0, at] += fs * dx
-                force_acc[q, 1, at] += fs * dy
-                force_acc[q, 2, at] += fs * dz
-            sums_ref[0] += tot
-            sums_ref[1] += tot_p
-            sums_ref[2] += tot_k
-
-        width = listed_ref.shape[-1]
-        unroll = 4 if width % 4 == 0 else 1
-
-        @pl.loop(0, width // unroll)
+                xi, yi, zi, hi, ei, qi, pi, si, wi = (own_cols[q, r, at] for r in range(COLS))
+                forces = None
+                for (xj, yj, zj, hj, ej, qj, pj, sj, wj), _ in others:
+                    dx, dy, dz = xi - xj, yi - yj, zi - zj
+                    r2 = dx * dx + dy * dy + dz * dz
+                    sig = hi + hj
+                    s2 = sig * sig
+                    s6 = s2 * s2 * s2
+                    soft = jnp.maximum(si, sj)
+                    p = jnp.maximum(pi, pj)
+                    r4 = r2 * r2
+                    inv = 1.0 / (s6 * soft + r4 * r2)
+                    u = lax.rsqrt(3.0 * r2 + soft)
+                    half = (qi * qj) * u
+                    ec = half + half
+                    half = half * (u * u)
+                    t = s6 * inv
+                    first = (ei * ej) * t
+                    second = first * t
+                    v = second - first
+                    m = second + v
+                    v = v + ec
+                    kk = m * t + half
+                    fs = jnp.minimum(wi, wj) * (m * (r4 * inv) + half)
+                    tot = tot + v
+                    tot_p = tot_p + p * v
+                    tot_k = tot_k + p * kk
+                    new = [fs * dx, fs * dy, fs * dz]
+                    forces = new if forces is None else [x + y for x, y in zip(forces, new)]
+                for k in range(3):
+                    force_acc[q, k, at] += forces[k]
+            for k, value in enumerate((tot, tot_p, tot_k)):
+                sums_ref[k] += value
+
+        @pl.loop(0, width // (together * groups))
         def _(step):
-            for k in range(unroll):
-                entry(step * unroll + k)
+            for k in range(groups):
+                turn(step * groups + k)
 
     folded = [jnp.sum(sums_ref[k], axis=0, keepdims=True) for k in range(3)]
     folded.append(jnp.zeros((5, LANES), jnp.float32))
@@ -346,7 +367,7 @@
                 )
                 for part in (high, low)
             )
-            force_ref[k, 0, 0, :, q * LANES : (q + 1) * LANES] = 2.0 * reduced[0:1]
+            force_ref[k, 0, 0, :, q * LANES : (q + 1) * LANES] = (2.0 * 3.0**0.5) * reduced[0:1]
 
     @pl.loop(1, total)
     def _(by):
@@ -411,9 +432,10 @@
             pltpu.VMEM((slots, 5, 1, atoms), f32),
             pltpu.VMEM((8, 2 * mig), f32),
             pltpu.VMEM((2, 8, 2 * mig), f32),
-            pltpu.VMEM((blocks, 7, LANES, LANES), f32),
+            pltpu.VMEM((blocks, COLS, LANES, LANES), f32),
             pltpu.VMEM((blocks, 3, LANES, LANES), f32),
             pltpu.VMEM((slots * blocks, 8, LANES), f32),
+            pltpu.VMEM((blocks, 3, 8, LANES), f32),
             pltpu.VMEM((3, 8, LANES), f32),
             pltpu.VMEM((8, LANES), f32),
             pltpu.VMEM((total, 8, LANES), f32),

time: 34.7 us -> 33 us (0.951)
  Pallas kernels: 33.2 us -> 31.6 us
    pallas_call x1, Pallas kernels: 32.1 us -> 30.4 us  [on_device(): pl.pallas_call(bound(step_kernel, sizes), name='step', out_shape=(pltpu.V...]
where the time goes in v3:
time: 33 us; the launch traced here: 32.9 us
  Pallas kernels  31.6 us (96%)
  between operations  1.29 us (4%)
    pallas_call x1, Pallas kernels, on_device(): pl.pallas_call(bound(step_kernel, sizes), name='step', out_shape=(pltpu.V...  30.4 us
    pallas_call x1, Pallas kernels, on_device(): pl.pallas_call(hand_over, name='hand_over', out_shape=(jax.ShapeDtypeStru...  1.13 us

profile of v3, /device:TPU:0, one launch (start us, length us, event | category | flops | bytes accessed | tf_op | source)
XLA Modules:
  0.0 32.9 jit_solution(7796995457637209879)
XLA Ops:
  1.3 30.4 %step.1 = (f32[3,1,1,1,768]{4,3,2,1,0:T(1,128)S(1)}, f32[8,128]{1,0:T(8,128)S(1)}) custom-call(f32[3]{0:T(128)} %refs_0_.1, f32[1]{0:T(128)S(6)} %copy.14.refs_1_, f32[32]{0:T(128)} %refs_2_.1, f32[32]{0:T(128)} %refs_3_.1, f32[32]{0:T(128)} %refs_4_.1, s32[6,1,16]{2,1,0:T(1,128)} %bitcast.1, s32[1,1,1,6]{3,2,1,0:T(1,128)} %refs_6_.1, ...), custom_call_target="tpu_custom_call" | custom-call | tf_op jit(solution)/shard_map/step/pallas_call | solution.py:422
  31.7 1.1 %hand_over.1 = (f32[3,1,1,1,768]{4,3,2,1,0:T(1,128)}, f32[1]{0:T(128)}, f32[1]{0:T(128)}) custom-call(f32[3,1,1,1,768]{4,3,2,1,0:T(1,128)S(1)} %get-tuple-element.5.force_in, f32[8,128]{1,0:T(8,128)S(1)} %get-tuple-element.6.tally_in), custom_call_target="tpu_custom_call" | custom-call | tf_op jit(solution)/shard_map/hand_over/pallas_call | solution.py:451

commit v4 on v3

--- a/solution.py
+++ b/solution.py
@@ -13,10 +13,15 @@
 LANES = 128
 MESH = pl.DeviceIdType.MESH
 COLS = 9
+ROWS = 5
 
 
 def steps_of(count):
     return {1: (0,), 2: (0, 1)}.get(count, (-1, 0, 1))
+
+
+def far_steps(count):
+    return {1: (), 2: (), 3: (), 4: (2,)}.get(count, (2, -2))
 
 
 def slot_step(step, count):
@@ -60,8 +65,8 @@
     ) = staged
     (
         ghost_ref,
-        outgoing,
-        incoming,
+        far_ref,
+        hot_ref,
         own_cols,
         force_acc,
         params,
@@ -69,8 +74,8 @@
         sums_ref,
         tile,
         gathered,
-        mig_send,
-        mig_recv,
+        far_send,
+        far_recv,
         send_sem,
         recv_sem,
         sum_send,
@@ -134,59 +139,78 @@
     slots_in = jnp.concatenate([leave[0:1], leave[1:2]], axis=1)
     slots_out = jnp.concatenate([leave[1:2], leave[0:1]], axis=1)
     place = lax.broadcasted_iota(jnp.int32, (atoms, 2 * mig), 0)
-    hot_in = (place == slots_in).astype(jnp.float32).astype(jnp.bfloat16)
     hot_out = (place == slots_out).astype(jnp.float32).astype(jnp.bfloat16)
     lane = lax.broadcasted_iota(jnp.int32, (8, 2 * mig), 1)
-    first = lax.broadcasted_iota(jnp.int32, (8, 2 * mig), 0) == 0
-    shift = jnp.where(first, jnp.where(lane < mig, edge[0], -edge[0]), 0.0)
+    deep = lax.broadcasted_iota(jnp.int32, (8, 2 * mig), 0)
+    shift = jnp.where(deep == 0, jnp.where(lane < mig, edge[0], -edge[0]), 0.0)
     leavers = joined(
         jnp.dot(thirds(payload).astype(jnp.bfloat16), hot_out, preferred_element_type=jnp.float32)
     )
-    outgoing[...] = leavers + shift
-
-    def spread(value):
-        return lax.dot_general(
-            value.astype(jnp.bfloat16),
-            hot_in,
-            (((1,), (1,)), ((), ())),
-            preferred_element_type=jnp.float32,
-        )
-
-    gone = spread(jnp.ones((8, 2 * mig), jnp.float32))
+    leavers = leavers + shift
+    blocks = atoms // LANES
+    body = blocks * ROWS
+    per_row = LANES // (2 * mig)
+    extras = -(-(ROWS + 1) // per_row)
+    for q in range(blocks):
+        for r in range(ROWS):
+            own[q * ROWS + r] = payload[r : r + 1, q * LANES : (q + 1) * LANES]
+    parts = [leavers[r : r + 1] for r in range(ROWS)] + [slots_in.astype(jnp.float32)]
+    parts += [parts[0] * 0.0] * (extras * per_row - ROWS - 1)
+    for r in range(extras):
+        own[body + r] = jnp.concatenate(parts[r * per_row : (r + 1) * per_row], axis=1)
 
     pl.semaphore_wait(barrier, total - 1)
-    moves = []
-    for side, by in ((0, 1), (1, -1)):
-        move = pltpu.make_async_remote_copy(
-            src_ref=outgoing,
-            dst_ref=incoming.at[side],
-            send_sem=mig_send.at[side],
-            recv_sem=mig_recv.at[side],
-            device_id=device((by, 0, 0)),
+
+    def passing(source, target, place, k):
+        return pltpu.make_async_remote_copy(
+            src_ref=source,
+            dst_ref=ghost_ref.at[place],
+            send_sem=send_sem.at[k],
+            recv_sem=recv_sem.at[place],
+            device_id=device(target),
             device_id_type=MESH,
         )
-        move.start()
-        moves.append(move)
-    for move in moves:
-        move.wait()
-    merged = jnp.where(lane < mig, incoming[1], incoming[0])
-    moved = jnp.where(gone > 0.5, joined(spread(thirds(merged))), payload)
-    for r in range(5):
-        own[r] = moved[r : r + 1]
-    copies = []
-    for k, o in enumerate(sorted(others, key=lambda o: -sum(map(abs, o)))):
-        copy = pltpu.make_async_remote_copy(
-            src_ref=own,
-            dst_ref=ghost_ref.at[slot(o)],
-            send_sem=send_sem.at[k],
-            recv_sem=recv_sem.at[k],
-            device_id=device(tuple(-x for x in o)),
+
+    fars = far_steps(nx)
+    ends = [(a, b, c) for a in fars for b in steps_of(ny) for c in steps_of(nz)]
+
+    def far_slot(a, b, c):
+        which = (2 - a) // 4 if len(fars) > 1 else 0
+        return (which * len(steps_of(ny)) + slot_step(b, ny)) * len(steps_of(nz)) + slot_step(c, nz)
+
+    def far_copy(k, target, here):
+        return pltpu.make_async_remote_copy(
+            src_ref=own.at[pl.ds(body, extras)],
+            dst_ref=far_ref.at[here],
+            send_sem=far_send.at[k],
+            recv_sem=far_recv.at[here],
+            device_id=device(target),
             device_id_type=MESH,
         )
+
+    far_copies = [
+        far_copy(k, (a, b, c), far_slot(-a if len(fars) > 1 else a, -b, -c))
+        for k, (a, b, c) in enumerate(ends)
+    ]
+    for copy in far_copies:
         copy.start()
-        copies.append((copy, slot(o)))
-
-    blocks = atoms // LANES
+
+    if nx > 2:
+        toward = 2 * lax.div(2 * me[0], nx) - 1
+        reach = [toward, -toward]
+    else:
+        reach = [x for x in steps_of(nx) if x]
+    sides = sorted((b for b in steps_of(ny)), key=lambda b: -abs(b))
+    plan = [(a, b) for a in reach for b in sides] + [(0, b) for b in sides if b]
+    up = [c for c in steps_of(nz) if c]
+    sends = []
+    for a, b in plan:
+        sends.append(passing(own, (a, b, 0), slot((-a, -b, 0)), len(sends)))
+        sends[-1].start()
+    for c in up:
+        sends.append(passing(own, (0, 0, -c), slot((0, 0, c)), len(sends)))
+        sends[-1].start()
+
     lam = coupling_ref[0]
     own_slot = slot((0, 0, 0))
     ones = jnp.ones((8, LANES), jnp.bfloat16)
@@ -210,16 +234,74 @@
     table_parts = thirds(table[:, :kinds]).astype(jnp.bfloat16)
     kind_row = lax.broadcasted_iota(jnp.int32, (kinds, atoms), 0).astype(jnp.float32)
 
-    def look_up(place):
-        onehot = (kind_row == ghost_ref[place, 3]).astype(jnp.float32).astype(jnp.bfloat16)
-        found = joined(jnp.dot(table_parts, onehot, preferred_element_type=jnp.float32))
-        rows = [ghost_ref[place, r] for r in range(3)]
-        rows += [found[0:3], ghost_ref[place, 4], found[3:4]]
-        whole = jnp.concatenate(rows, axis=0)
+    low_side = jnp.where(lax.broadcasted_iota(jnp.int32, (1, 2 * mig), 1) < mig, 1, -1)
+    atom_lane = lax.broadcasted_iota(jnp.int32, (2 * mig, atoms), 1).astype(jnp.float32)
+    one_row = jnp.ones((1, 2 * mig), jnp.float32)
+
+    def extra_rows(a, b, c):
+        far = not isinstance(a, int) or abs(a) == 2
+        if far and fars:
+            found = [far_ref[far_slot(a, b, c), r] for r in range(extras)]
+        else:
+            if far:
+                a = -a // 2 if nx == 3 else 0
+            found = [ghost_ref[slot((a, b, c)), body + r] for r in range(extras)]
+        return [
+            found[r // per_row][:, (r % per_row) * 2 * mig : (r % per_row + 1) * 2 * mig]
+            for r in range(ROWS + 1)
+        ]
+
+    def prepare(a, b, c):
+        place = slot((a, b, c))
+        rows = [
+            jnp.concatenate([ghost_ref[place, q * ROWS + r] for q in range(blocks)], axis=1)
+            for r in range(ROWS)
+        ]
+        found = joined(
+            jnp.dot(
+                table_parts,
+                (kind_row == rows[3]).astype(jnp.float32).astype(jnp.bfloat16),
+                preferred_element_type=jnp.float32,
+            )
+        )
+        whole = jnp.concatenate(rows[0:3] + [found[0:3], rows[4], found[3:4]], axis=0)
         for q in range(blocks):
             params[place * blocks + q] = whole[:, q * LANES : (q + 1) * LANES]
-
-    look_up(own_slot)
+        at = ROWS % per_row
+        slots_here = ghost_ref[place, body + ROWS // per_row][:, at * 2 * mig : (at + 1) * 2 * mig]
+        column = jnp.broadcast_to(slots_here, (8, 2 * mig)).T[:, 0:1]
+        hot = jnp.broadcast_to(column, (2 * mig, atoms)) == atom_lane
+        hot_ref[place] = hot.astype(jnp.float32).astype(jnp.bfloat16)
+
+    def patch(a, b, c):
+        place = slot((a, b, c))
+        if isinstance(a, int) and a == 0:
+            near, away = extra_rows(1, b, c), extra_rows(-1, b, c)
+            pick = low_side > 0
+        else:
+            near, away = extra_rows(2 * a, b, c), extra_rows(0, b, c)
+            pick = low_side * a > 0
+        rows = [jnp.where(pick, x, y) for x, y in zip(near[:ROWS], away[:ROWS])]
+        found = joined(
+            jnp.dot(
+                table_parts,
+                (kind_row[:, : 2 * mig] == rows[3]).astype(jnp.float32).astype(jnp.bfloat16),
+                preferred_element_type=jnp.float32,
+            )
+        )
+        whole = jnp.concatenate(rows[0:3] + [found[0:3], rows[4], one_row], axis=0)
+        spread = joined(
+            jnp.dot(
+                thirds(whole).astype(jnp.bfloat16),
+                hot_ref[place],
+                preferred_element_type=jnp.float32,
+            )
+        )
+        for q in range(blocks):
+            new = spread[:, q * LANES : (q + 1) * LANES]
+            at = place * blocks + q
+            params[at] = jnp.where(new[7:8] > 0.5, new, params[at])
+
     picks = (
         lax.broadcasted_iota(jnp.int32, (24, COLS * LANES), 0) % 8
         == lax.broadcasted_iota(jnp.int32, (24, COLS * LANES), 1) // LANES
@@ -229,35 +311,84 @@
         return [soft_base + (soft_alpha * lam) * flag, 1.0 - lam * flag]
 
     deep = lax.broadcasted_iota(jnp.int32, (8, LANES), 0)
-    for q in range(blocks):
-        rows = params[own_slot * blocks + q]
-        rows = jnp.concatenate([rows[0:5], rows[5:6] * (0.5 * coulomb), rows[6:8]], axis=0)
-        cols = thirds(rows).T.astype(jnp.bfloat16)
-        wide = jnp.dot(cols, picks, preferred_element_type=jnp.float32)
-        for r in range(7):
-            own_cols[q, r] = wide[:, r * LANES : (r + 1) * LANES]
-        for r, col in enumerate(graded(own_cols[q, 6])):
-            own_cols[q, 7 + r] = col
-        flag = rows[6:7]
-        (soft,) = graded(flag)[:1]
-        ratio = 1.0 / soft
-        root = lax.rsqrt(soft)
-        plain = params[own_slot * blocks + q][5:6]
-        electric = (coulomb * root) * plain * plain
-        first = rows[4:5] * rows[4:5] * ratio
-        second = first * ratio
-        alone = second - first
-        slope = (second + alone) * ratio + 0.5 * electric * (root * root)
-        alone = alone + electric
-        for k, value in enumerate((alone, flag * alone, flag * slope)):
-            self_ref[q, k] = jnp.where(deep == 0, value, 0.0)
+    def own_side():
+        for q in range(blocks):
+            rows = params[own_slot * blocks + q]
+            rows = jnp.concatenate([rows[0:5], rows[5:6] * (0.5 * coulomb), rows[6:8]], axis=0)
+            cols = thirds(rows).T.astype(jnp.bfloat16)
+            wide = jnp.dot(cols, picks, preferred_element_type=jnp.float32)
+            for r in range(7):
+                own_cols[q, r] = wide[:, r * LANES : (r + 1) * LANES]
+            for r, col in enumerate(graded(own_cols[q, 6])):
+                own_cols[q, 7 + r] = col
+            flag = rows[6:7]
+            (soft,) = graded(flag)[:1]
+            ratio = 1.0 / soft
+            root = lax.rsqrt(soft)
+            plain = params[own_slot * blocks + q][5:6]
+            electric = (coulomb * root) * plain * plain
+            first = rows[4:5] * rows[4:5] * ratio
+            second = first * ratio
+            alone = second - first
+            slope = (second + alone) * ratio + 0.5 * electric * (root * root)
+            alone = alone + electric
+            for k, value in enumerate((alone, flag * alone, flag * slope)):
+                self_ref[q, k] = jnp.where(deep == 0, value, 0.0)
+
     for q in range(blocks):
         for k in range(3):
             force_acc[q, k] = jnp.zeros((LANES, LANES), jnp.float32)
 
-    for copy, place in copies:
-        copy.wait()
-        look_up(place)
+    def arrive(a, b):
+        here = slot((a, b, 0))
+        passing(own, (a, b, 0), here, 0).wait_recv()
+        for c in up:
+            sends.append(passing(ghost_ref.at[here], (0, 0, -c), slot((a, b, c)), len(sends)))
+            sends[-1].start()
+
+    def across(a, b):
+        for c in up:
+            passing(own, (0, 0, -c), slot((a, b, c)), 0).wait_recv()
+            prepare(a, b, c)
+
+    nearest = sides[::-1]
+    prepare(0, 0, 0)
+    for b in nearest:
+        if b:
+            arrive(0, b)
+            prepare(0, b, 0)
+    across(0, 0)
+    for a in reach[1:]:
+        for b in nearest:
+            arrive(a, b)
+            prepare(a, b, 0)
+    for b in nearest:
+        if b:
+            across(0, b)
+    for a in reach[1:]:
+        for b in nearest:
+            across(a, b)
+    for o in ends:
+        far_copy(0, o, far_slot(*o)).wait_recv()
+    for a in reach[1:]:
+        for b in nearest:
+            for c in steps_of(nz):
+                patch(a, b, c)
+    for a in reach[:1]:
+        for b in nearest:
+            arrive(a, b)
+    for b in nearest:
+        for a in reach[:1]:
+            prepare(a, b, 0)
+            patch(a, b, 0)
+        patch(0, b, 0)
+    own_side()
+    for b in nearest:
+        for a in reach[:1]:
+            across(a, b)
+        for c in up:
+            for a in [0] + reach[:1]:
+                patch(a, b, c)
 
     width = listed_ref.shape[-1]
     together = 2 if width % 2 == 0 else 1
@@ -336,9 +467,15 @@
             for k in range(groups):
                 turn(step * groups + k)
 
-    folded = [jnp.sum(sums_ref[k], axis=0, keepdims=True) for k in range(3)]
-    folded.append(jnp.zeros((5, LANES), jnp.float32))
-    mine = jnp.concatenate(folded, axis=0)
+    part = LANES // 4
+
+    def narrowed(row):
+        row = row + pltpu.roll(row, LANES // 2, 1)
+        return row + pltpu.roll(row, part, 1)
+
+    folded = [narrowed(jnp.sum(sums_ref[k], axis=0, keepdims=True)) for k in range(3)]
+    lane = lax.broadcasted_iota(jnp.int32, (1, LANES), 1)
+    mine = jnp.where(lane < part, folded[0], jnp.where(lane < 2 * part, folded[1], folded[2]))
     tile[...] = mine
     gathered[my_id] = mine
 
@@ -369,12 +506,17 @@
             )
             force_ref[k, 0, 0, :, q * LANES : (q + 1) * LANES] = (2.0 * 3.0**0.5) * reduced[0:1]
 
+    for copy in sends + far_copies:
+        copy.wait_send()
+
     @pl.loop(1, total)
     def _(by):
         share(by).wait()
 
     summed = jnp.sum(gathered[...], axis=0)
-    parts = [jnp.sum(summed[k : k + 1]) for k in range(3)]
+    parts = [
+        jnp.sum(jnp.where(lax.div(lane, part) == k, summed, 0.0)) for k in range(3)
+    ]
     scale = 0.5 / float(atoms * total)
     rows = lax.broadcasted_iota(jnp.int32, (8, LANES), 0)
     energy = scale * (parts[0] - lam * parts[1])
@@ -396,6 +538,9 @@
     atoms = fraction.shape[-1]
     mig = leaving.shape[-1]
     slots = len(steps_of(nx)) * len(steps_of(ny)) * len(steps_of(nz))
+    planar = len(steps_of(ny)) * len(steps_of(nz))
+    far_slots = max(len(far_steps(nx)), 1) * planar
+    extras = -(-(ROWS + 1) // (LANES // (2 * mig)))
     smem = pl.BlockSpec(memory_space=pltpu.SMEM)
     vmem = pl.BlockSpec(memory_space=pltpu.VMEM)
     f32 = jnp.float32
@@ -429,18 +574,18 @@
             *(pltpu.SMEM(x.shape, x.dtype) for x in arrays[:7]),
             *(pltpu.VMEM(x.shape, x.dtype) for x in arrays[7:]),
             dma((11,)),
-            pltpu.VMEM((slots, 5, 1, atoms), f32),
-            pltpu.VMEM((8, 2 * mig), f32),
-            pltpu.VMEM((2, 8, 2 * mig), f32),
+            pltpu.VMEM((slots, blocks * ROWS + extras, 1, LANES), f32),
+            pltpu.VMEM((far_slots, extras, 1, LANES), f32),
+            pltpu.VMEM((slots, 2 * mig, atoms), jnp.bfloat16),
             pltpu.VMEM((blocks, COLS, LANES, LANES), f32),
             pltpu.VMEM((blocks, 3, LANES, LANES), f32),
             pltpu.VMEM((slots * blocks, 8, LANES), f32),
             pltpu.VMEM((blocks, 3, 8, LANES), f32),
             pltpu.VMEM((3, 8, LANES), f32),
-            pltpu.VMEM((8, LANES), f32),
-            pltpu.VMEM((total, 8, LANES), f32),
-            dma((2,)),
-            dma((2,)),
+            pltpu.VMEM((1, LANES), f32),
+            pltpu.VMEM((total, 1, LANES), f32),
+            dma((far_slots,)),
+            dma((far_slots,)),
             dma((slots,)),
             dma((slots,)),
             dma((total,)),

time: 33 us -> 31.8 us (0.964)
  Pallas kernels: 31.6 us -> 30.3 us
    pallas_call x1, Pallas kernels: 30.4 us -> 29.2 us  [on_device(): pl.pallas_call(bound(step_kernel, sizes), name='step', out_shape=(pltpu.V...]
where the time goes in v4:
time: 31.8 us; the launch traced here: 31.6 us
  Pallas kernels  30.3 us (95%)
  between operations  1.29 us (4%)
    pallas_call x1, Pallas kernels, on_device(): pl.pallas_call(bound(step_kernel, sizes), name='step', out_shape=(pltpu.V...  29.2 us
    pallas_call x1, Pallas kernels, on_device(): pl.pallas_call(hand_over, name='hand_over', out_shape=(jax.ShapeDtypeStru...  1.13 us

profile of v4, /device:TPU:0, one launch (start us, length us, event | category | flops | bytes accessed | tf_op | source)
XLA Modules:
  0.0 31.6 jit_solution(14983668708352814127)
XLA Ops:
  1.3 29.2 %step.1 = (f32[3,1,1,1,768]{4,3,2,1,0:T(1,128)S(1)}, f32[8,128]{1,0:T(8,128)S(1)}) custom-call(f32[3]{0:T(128)} %refs_0_.1, f32[1]{0:T(128)S(6)} %copy.14.refs_1_, f32[32]{0:T(128)} %refs_2_.1, f32[32]{0:T(128)} %refs_3_.1, f32[32]{0:T(128)} %refs_4_.1, s32[6,1,16]{2,1,0:T(1,128)} %bitcast.1, s32[1,1,1,6]{3,2,1,0:T(1,128)} %refs_6_.1, ...), custom_call_target="tpu_custom_call" | custom-call | tf_op jit(solution)/shard_map/step/pallas_call | solution.py:567
  30.5 1.1 %hand_over.1 = (f32[3,1,1,1,768]{4,3,2,1,0:T(1,128)}, f32[1]{0:T(128)}, f32[1]{0:T(128)}) custom-call(f32[3,1,1,1,768]{4,3,2,1,0:T(1,128)S(1)} %get-tuple-element.5.force_in, f32[8,128]{1,0:T(8,128)S(1)} %get-tuple-element.6.tally_in), custom_call_target="tpu_custom_call" | custom-call | tf_op jit(solution)/shard_map/hand_over/pallas_call | solution.py:596

commit v5 on v4

--- a/solution.py
+++ b/solution.py
@@ -71,6 +71,7 @@
         force_acc,
         params,
         self_ref,
+        slopes,
         sums_ref,
         tile,
         gathered,
@@ -394,12 +395,8 @@
     together = 2 if width % 2 == 0 else 1
     groups = 8 if width % (8 * together) == 0 else 1
 
-    def entry(q, e):
+    def listed_rows(q, e):
         listed = listed_ref[q, 0, e]
-        left = jnp.minimum(jnp.maximum(count_ref[0, 0, 0, q] - e, 0), 1)
-        used = left.astype(jnp.float32)
-        apart = jnp.abs(listed - (13 * blocks + q))
-        itself = ((1 - jnp.minimum(apart, 1)) * left).astype(jnp.float32)
         image = lax.div(listed, blocks)
         a = lax.div(image, 9) - 1
         b = lax.rem(lax.div(image, 3), 3) - 1
@@ -408,15 +405,23 @@
             slot_step(a, nx) * len(steps_of(ny)) + slot_step(b, ny)
         ) * len(steps_of(nz)) + slot_step(c, nz)
         other = params[where_from * blocks + lax.rem(listed, blocks)]
+        return other, [x.astype(jnp.float32) * y for x, y in zip((a, b, c), edge)], listed
+
+    def entry(q, e):
+        other, step_by, listed = listed_rows(q, e)
+        left = jnp.minimum(jnp.maximum(count_ref[0, 0, 0, q] - e, 0), 1)
+        used = left.astype(jnp.float32)
+        apart = jnp.abs(listed - (13 * blocks + q))
+        itself = ((1 - jnp.minimum(apart, 1)) * left).astype(jnp.float32)
         rows = []
         for r in range(7):
             row = other[r : r + 1]
             if r < 3:
-                row = row + (a, b, c)[r].astype(jnp.float32) * edge[r]
+                row = row + step_by[r]
             if 4 <= r < 6:
                 row = row * used
             rows.append(row)
-        rows += graded(rows[6])
+        rows.append(graded(rows[6])[0])
         return [jnp.broadcast_to(row, (8, LANES)) for row in rows], itself
 
     @pl.loop(0, blocks)
@@ -428,9 +433,8 @@
             )
             for g in range(LANES // 8):
                 at = pl.ds(g * 8, 8)
-                xi, yi, zi, hi, ei, qi, pi, si, wi = (own_cols[q, r, at] for r in range(COLS))
-                forces = None
-                for (xj, yj, zj, hj, ej, qj, pj, sj, wj), _ in others:
+                xi, yi, zi, hi, ei, qi, pi, si = (own_cols[q, r, at] for r in range(8))
+                for k, ((xj, yj, zj, hj, ej, qj, pj, sj), _) in enumerate(others):
                     dx, dy, dz = xi - xj, yi - yj, zi - zj
                     r2 = dx * dx + dy * dy + dz * dz
                     sig = hi + hj
@@ -451,14 +455,10 @@
                     m = second + v
                     v = v + ec
                     kk = m * t + half
-                    fs = jnp.minimum(wi, wj) * (m * (r4 * inv) + half)
+                    slopes[q, step * together + k, at] = m * (r4 * inv) + half
                     tot = tot + v
                     tot_p = tot_p + p * v
                     tot_k = tot_k + p * kk
-                    new = [fs * dx, fs * dy, fs * dz]
-                    forces = new if forces is None else [x + y for x, y in zip(forces, new)]
-                for k in range(3):
-                    force_acc[q, k, at] += forces[k]
             for k, value in enumerate((tot, tot_p, tot_k)):
                 sums_ref[k] += value
 
@@ -492,6 +492,31 @@
     @pl.loop(1, total)
     def _(by):
         share(by).start()
+
+    joint = 4 if width % 4 == 0 else 1
+
+    @pl.loop(0, blocks)
+    def _(q):
+        def sweep(step):
+            others = []
+            for k in range(joint):
+                other, step_by, _ = listed_rows(q, step * joint + k)
+                rows = [other[r : r + 1] + step_by[r] for r in range(3)]
+                rows.append(graded(other[6:7])[1])
+                others.append([jnp.broadcast_to(row, (8, LANES)) for row in rows])
+            for g in range(LANES // 8):
+                at = pl.ds(g * 8, 8)
+                xi, yi, zi, wi = (own_cols[q, r, at] for r in (0, 1, 2, 8))
+                forces = None
+                for k, (xj, yj, zj, wj) in enumerate(others):
+                    fs = slopes[q, step * joint + k, at] * jnp.minimum(wi, wj)
+                    new = [fs * (xi - xj), fs * (yi - yj), fs * (zi - zj)]
+                    forces = new if forces is None else [x + y for x, y in zip(forces, new)]
+                for k in range(3):
+                    force_acc[q, k, at] += forces[k]
+
+        for step in range(width // joint):
+            sweep(step)
 
     for q in range(blocks):
         for k in range(3):
@@ -581,6 +606,7 @@
             pltpu.VMEM((blocks, 3, LANES, LANES), f32),
             pltpu.VMEM((slots * blocks, 8, LANES), f32),
             pltpu.VMEM((blocks, 3, 8, LANES), f32),
+            pltpu.VMEM((blocks, neighbours.shape[-1], LANES, LANES), f32),
             pltpu.VMEM((3, 8, LANES), f32),
             pltpu.VMEM((1, LANES), f32),
             pltpu.VMEM((total, 1, LANES), f32),

time: 31.8 us -> 30.2 us (0.950)
  Pallas kernels: 30.3 us -> 28.7 us
    pallas_call x1, Pallas kernels: 29.2 us -> 27.6 us  [on_device(): pl.pallas_call(bound(step_kernel, sizes), name='step', out_shape=(pltpu.V...]
where the time goes in v5:
time: 30.2 us; the launch traced here: 30 us
  Pallas kernels  28.7 us (95%)
  between operations  1.29 us (4%)
    pallas_call x1, Pallas kernels, on_device(): pl.pallas_call(bound(step_kernel, sizes), name='step', out_shape=(pltpu.V...  27.6 us
    pallas_call x1, Pallas kernels, on_device(): pl.pallas_call(hand_over, name='hand_over', out_shape=(jax.ShapeDtypeStru...  1.13 us

profile of v5, /device:TPU:0, one launch (start us, length us, event | category | flops | bytes accessed | tf_op | source)
XLA Modules:
  0.0 30.0 jit_solution(17591585010970226816)
XLA Ops:
  1.3 27.6 %step.1 = (f32[3,1,1,1,768]{4,3,2,1,0:T(1,128)S(1)}, f32[8,128]{1,0:T(8,128)S(1)}) custom-call(f32[3]{0:T(128)} %refs_0_.1, f32[1]{0:T(128)S(6)} %copy.14.refs_1_, f32[32]{0:T(128)} %refs_2_.1, f32[32]{0:T(128)} %refs_3_.1, f32[32]{0:T(128)} %refs_4_.1, s32[6,1,16]{2,1,0:T(1,128)} %bitcast.1, s32[1,1,1,6]{3,2,1,0:T(1,128)} %refs_6_.1, ...), custom_call_target="tpu_custom_call" | custom-call | tf_op jit(solution)/shard_map/step/pallas_call | solution.py:592
  28.9 1.1 %hand_over.1 = (f32[3,1,1,1,768]{4,3,2,1,0:T(1,128)}, f32[1]{0:T(128)}, f32[1]{0:T(128)}) custom-call(f32[3,1,1,1,768]{4,3,2,1,0:T(1,128)S(1)} %get-tuple-element.5.force_in, f32[8,128]{1,0:T(8,128)S(1)} %get-tuple-element.6.tally_in), custom_call_target="tpu_custom_call" | custom-call | tf_op jit(solution)/shard_map/hand_over/pallas_call | solution.py:622

commit v6 on v5

--- a/solution.py
+++ b/solution.py
@@ -392,8 +392,8 @@
                 patch(a, b, c)
 
     width = listed_ref.shape[-1]
-    together = 2 if width % 2 == 0 else 1
-    groups = 8 if width % (8 * together) == 0 else 1
+    together = 1 if width % 1 == 0 else 1
+    groups = 16 if width % (16 * together) == 0 else 1
 
     def listed_rows(q, e):
         listed = listed_ref[q, 0, e]
@@ -438,24 +438,23 @@
                     dx, dy, dz = xi - xj, yi - yj, zi - zj
                     r2 = dx * dx + dy * dy + dz * dz
                     sig = hi + hj
-                    s2 = sig * sig
-                    s6 = s2 * s2 * s2
+                    is2 = 1.0 / (sig * sig)
                     soft = jnp.maximum(si, sj)
                     p = jnp.maximum(pi, pj)
-                    r4 = r2 * r2
-                    inv = 1.0 / (s6 * soft + r4 * r2)
+                    x = r2 * is2
+                    x2 = x * x
+                    t = 1.0 / (soft + x2 * x)
                     u = lax.rsqrt(3.0 * r2 + soft)
                     half = (qi * qj) * u
                     ec = half + half
                     half = half * (u * u)
-                    t = s6 * inv
                     first = (ei * ej) * t
                     second = first * t
                     v = second - first
-                    m = second + v
+                    mt = (second + v) * t
                     v = v + ec
-                    kk = m * t + half
-                    slopes[q, step * together + k, at] = m * (r4 * inv) + half
+                    kk = mt + half
+                    slopes[q, step * together + k, at] = mt * (x2 * is2) + half
                     tot = tot + v
                     tot_p = tot_p + p * v
                     tot_k = tot_k + p * kk

time: 30.2 us -> 29.8 us (0.987)
  Pallas kernels: 28.7 us -> 28.3 us
    pallas_call x1, Pallas kernels: 27.6 us -> 27.2 us  [on_device(): pl.pallas_call(bound(step_kernel, sizes), name='step', out_shape=(pltpu.V...]
where the time goes in v6:
time: 29.8 us; the launch traced here: 29.6 us
  Pallas kernels  28.3 us (95%)
  between operations  1.29 us (4%)
    pallas_call x1, Pallas kernels, on_device(): pl.pallas_call(bound(step_kernel, sizes), name='step', out_shape=(pltpu.V...  27.2 us
    pallas_call x1, Pallas kernels, on_device(): pl.pallas_call(hand_over, name='hand_over', out_shape=(jax.ShapeDtypeStru...  1.13 us

profile of v6, /device:TPU:0, one launch (start us, length us, event | category | flops | bytes accessed | tf_op | source)
XLA Modules:
  0.0 29.6 jit_solution(13268906595116169943)
XLA Ops:
  1.3 27.2 %step.1 = (f32[3,1,1,1,768]{4,3,2,1,0:T(1,128)S(1)}, f32[8,128]{1,0:T(8,128)S(1)}) custom-call(f32[3]{0:T(128)} %refs_0_.1, f32[1]{0:T(128)S(6)} %copy.14.refs_1_, f32[32]{0:T(128)} %refs_2_.1, f32[32]{0:T(128)} %refs_3_.1, f32[32]{0:T(128)} %refs_4_.1, s32[6,1,16]{2,1,0:T(1,128)} %bitcast.1, s32[1,1,1,6]{3,2,1,0:T(1,128)} %refs_6_.1, ...), custom_call_target="tpu_custom_call" | custom-call | tf_op jit(solution)/shard_map/step/pallas_call | solution.py:591
  28.5 1.1 %hand_over.1 = (f32[3,1,1,1,768]{4,3,2,1,0:T(1,128)}, f32[1]{0:T(128)}, f32[1]{0:T(128)}) custom-call(f32[3,1,1,1,768]{4,3,2,1,0:T(1,128)S(1)} %get-tuple-element.5.force_in, f32[8,128]{1,0:T(8,128)S(1)} %get-tuple-element.6.tally_in), custom_call_target="tpu_custom_call" | custom-call | tf_op jit(solution)/shard_map/hand_over/pallas_call | solution.py:621

commit v7 on v6

--- a/solution.py
+++ b/solution.py
@@ -424,47 +424,48 @@
         rows.append(graded(rows[6])[0])
         return [jnp.broadcast_to(row, (8, LANES)) for row in rows], itself
 
-    @pl.loop(0, blocks)
-    def _(q):
-        def turn(step):
-            others = [entry(q, step * together + k) for k in range(together)]
-            tot, tot_p, tot_k = (
-                sum(-itself * self_ref[q, k] for _, itself in others) for k in range(3)
-            )
-            for g in range(LANES // 8):
-                at = pl.ds(g * 8, 8)
-                xi, yi, zi, hi, ei, qi, pi, si = (own_cols[q, r, at] for r in range(8))
-                for k, ((xj, yj, zj, hj, ej, qj, pj, sj), _) in enumerate(others):
-                    dx, dy, dz = xi - xj, yi - yj, zi - zj
-                    r2 = dx * dx + dy * dy + dz * dz
-                    sig = hi + hj
-                    is2 = 1.0 / (sig * sig)
-                    soft = jnp.maximum(si, sj)
-                    p = jnp.maximum(pi, pj)
-                    x = r2 * is2
-                    x2 = x * x
-                    t = 1.0 / (soft + x2 * x)
-                    u = lax.rsqrt(3.0 * r2 + soft)
-                    half = (qi * qj) * u
-                    ec = half + half
-                    half = half * (u * u)
-                    first = (ei * ej) * t
-                    second = first * t
-                    v = second - first
-                    mt = (second + v) * t
-                    v = v + ec
-                    kk = mt + half
-                    slopes[q, step * together + k, at] = mt * (x2 * is2) + half
-                    tot = tot + v
-                    tot_p = tot_p + p * v
-                    tot_k = tot_k + p * kk
-            for k, value in enumerate((tot, tot_p, tot_k)):
-                sums_ref[k] += value
-
-        @pl.loop(0, width // (together * groups))
-        def _(step):
-            for k in range(groups):
-                turn(step * groups + k)
+    def turn(q, step):
+        others = [entry(q, step * together + k) for k in range(together)]
+        tot, tot_p, tot_k = (
+            sum(-itself * self_ref[q, k] for _, itself in others) for k in range(3)
+        )
+        for g in range(LANES // 8):
+            at = pl.ds(g * 8, 8)
+            xi, yi, zi, hi, ei, qi, pi, si = (own_cols[q, r, at] for r in range(8))
+            for k, ((xj, yj, zj, hj, ej, qj, pj, sj), _) in enumerate(others):
+                dx, dy, dz = xi - xj, yi - yj, zi - zj
+                r2 = dx * dx + dy * dy + dz * dz
+                sig = hi + hj
+                is2 = 1.0 / (sig * sig)
+                soft = jnp.maximum(si, sj)
+                p = jnp.maximum(pi, pj)
+                x = r2 * is2
+                x2 = x * x
+                t = 1.0 / (soft + x2 * x)
+                u = lax.rsqrt(3.0 * r2 + soft)
+                half = (qi * qj) * u
+                ec = half + half
+                half = half * (u * u)
+                first = (ei * ej) * t
+                second = first * t
+                v = second - first
+                mt = (second + v) * t
+                v = v + ec
+                kk = mt + half
+                slopes[q, step * together + k, at] = mt * (x2 * is2) + half
+                tot = tot + v
+                tot_p = tot_p + p * v
+                tot_k = tot_k + p * kk
+        for k, value in enumerate((tot, tot_p, tot_k)):
+            sums_ref[k] += value
+
+    joined_blocks = 2 if blocks % 2 == 0 else 1
+
+    @pl.loop(0, blocks // joined_blocks)
+    def _(some):
+        for k in range(joined_blocks):
+            for step in range(width // together):
+                turn(some * joined_blocks + k, step)
 
     part = LANES // 4
 
@@ -488,9 +489,14 @@
             device_id_type=MESH,
         )
 
-    @pl.loop(1, total)
-    def _(by):
-        share(by).start()
+    if total <= 32:
+        for by in range(1, total):
+            share(by).start()
+    else:
+
+        @pl.loop(1, total)
+        def _(by):
+            share(by).start()
 
     joint = 4 if width % 4 == 0 else 1
 
@@ -538,14 +544,13 @@
         share(by).wait()
 
     summed = jnp.sum(gathered[...], axis=0)
-    parts = [
-        jnp.sum(jnp.where(lax.div(lane, part) == k, summed, 0.0)) for k in range(3)
-    ]
+    third = lax.div(lane, part)
     scale = 0.5 / float(atoms * total)
-    rows = lax.broadcasted_iota(jnp.int32, (8, LANES), 0)
-    energy = scale * (parts[0] - lam * parts[1])
-    dhdl = -scale * (parts[1] + (0.5 * (1.0 - lam)) * parts[2])
-    tally_ref[...] = jnp.where(rows == 0, energy, dhdl)
+    first = jnp.where(third == 0, scale, jnp.where(third == 1, -scale * lam, 0.0))
+    second = jnp.where(third == 1, -scale, (-0.5 * scale) * (1.0 - lam))
+    second = jnp.where(third == 0, 0.0, jnp.where(third == 3, 0.0, second))
+    both = jnp.concatenate([summed * first, summed * second], axis=0)
+    tally_ref[...] = jnp.broadcast_to(jnp.sum(both, axis=1, keepdims=True), (2, LANES))
 
 
 def hand_over(force_in, tally_in, force_ref, energy_ref, dhdl_ref, sem):
@@ -591,7 +596,7 @@
     forces, tally = pl.pallas_call(
         bound(step_kernel, sizes),
         name="step",
-        out_shape=(pltpu.VMEM(fraction.shape, f32), pltpu.VMEM((8, LANES), f32)),
+        out_shape=(pltpu.VMEM(fraction.shape, f32), pltpu.VMEM((2, LANES), f32)),
         in_specs=[pl.BlockSpec(memory_space=pl.ANY)] * 11,
         out_specs=(vmem, vmem),
         scratch_shapes=[

time: 29.8 us -> 29.5 us (0.990)
  Pallas kernels: 28.3 us -> 28 us
    pallas_call x1, Pallas kernels: 27.2 us -> 26.9 us  [on_device(): pl.pallas_call(bound(step_kernel, sizes), name='step', out_shape=(pltpu.V...]
where the time goes in v7:
time: 29.5 us; the launch traced here: 29.3 us
  Pallas kernels  28 us (95%)
  between operations  1.29 us (4%)
    pallas_call x1, Pallas kernels, on_device(): pl.pallas_call(bound(step_kernel, sizes), name='step', out_shape=(pltpu.V...  26.9 us
    pallas_call x1, Pallas kernels, on_device(): pl.pallas_call(hand_over, name='hand_over', out_shape=(jax.ShapeDtypeStru...  1.13 us

profile of v7, /device:TPU:0, one launch (start us, length us, event | category | flops | bytes accessed | tf_op | source)
XLA Modules:
  0.0 29.3 jit_solution(2972700745183124371)
XLA Ops:
  1.3 26.9 %step.1 = (f32[3,1,1,1,768]{4,3,2,1,0:T(1,128)S(1)}, f32[2,128]{1,0:T(2,128)S(1)}) custom-call(f32[3]{0:T(128)} %refs_0_.1, f32[1]{0:T(128)S(6)} %copy.14.refs_1_, f32[32]{0:T(128)} %refs_2_.1, f32[32]{0:T(128)} %refs_3_.1, f32[32]{0:T(128)} %refs_4_.1, s32[6,1,16]{2,1,0:T(1,128)} %bitcast.1, s32[1,1,1,6]{3,2,1,0:T(1,128)} %refs_6_.1, ...), custom_call_target="tpu_custom_call" | custom-call | tf_op jit(solution)/shard_map/step/pallas_call | solution.py:596
  28.2 1.1 %hand_over.1 = (f32[3,1,1,1,768]{4,3,2,1,0:T(1,128)}, f32[1]{0:T(128)}, f32[1]{0:T(128)}) custom-call(f32[3,1,1,1,768]{4,3,2,1,0:T(1,128)S(1)} %get-tuple-element.5.force_in, f32[2,128]{1,0:T(2,128)S(1)} %get-tuple-element.6.tally_in), custom_call_target="tpu_custom_call" | custom-call | tf_op jit(solution)/shard_map/hand_over/pallas_call | solution.py:626
